TPU v7x, 8 devices: a whole 2x2x1 slice. The times are simulated.
8 devices in a mesh: dp: 1 (over z), tp: 2 (over y), ep: 4 (over x, core).
Axes of the slice: x: 2, y: 2, z: 1, core: 2. Of those that a mesh axis runs over, the one named last changes fastest.
Arguments:
- tokens: bfloat16 [1024, 1024], P(('dp', 'ep'))
- grad_out: bfloat16 [1024, 1024], P(('dp', 'ep'))
- w_router: bfloat16 [1024, 8], replicated
- w_in: bfloat16 [8, 1024, 4096], P('ep', None, 'tp')
- w_out: bfloat16 [8, 4096, 1024], P('ep', 'tp')
- expert_ids: int32 [1024], P(('dp', 'ep'))
Outputs:
- output 1: bfloat16 [1024, 1024], P(('dp', 'ep'))
- output 2: bfloat16 [1024, 1024], P(('dp', 'ep'))
- output 3: float32 [8, 1024, 4096], P(('dp', 'ep'), None, 'tp')
- output 4: float32 [8, 4096, 1024], P(('dp', 'ep'), 'tp')
- output 5: float32 [1024, 8], P('dp')
All inputs are finite; a program needn't handle non-finite values.
Results may differ from a plain program's by a relative error of at most 0.00633399.
Values are sent between devices in bfloat16 or wider.
A program may use at most 1 GiB of HBM per device.

v0:
```python
import jax
import jax.numpy as jnp
from jax import lax
from jax.experimental import pallas as pl
from jax.experimental.pallas import tpu as pltpu
from jax.sharding import PartitionSpec as P


MESH = pl.DeviceIdType.MESH
F32, BF16 = jnp.float32, jnp.bfloat16
CONTRACT_LAST = (((1,), (1,)), ((), ()))
CONTRACT_FIRST = (((0,), (0,)), ((), ()))
GELU_C = 0.7978845608028654
GELU_K = 0.044715


def mm(a, b, dims=(((1,), (0,)), ((), ()))):
    return lax.dot_general(a, b, dims, preferred_element_type=F32)


def ep_partners():
    ep = lax.axis_index("ep")
    cx, cc = ep // 2, ep % 2
    return [ep, 2 * cx + (1 - cc), 2 * (1 - cx) + cc, 2 * (1 - cx) + (1 - cc)]


def route(idx_row, capacity, n_experts, stride):
    n = idx_row.shape[1]
    expert = lax.broadcasted_iota(jnp.int32, (n_experts, n), 0)
    hot = jnp.where(expert == idx_row, 1.0, 0.0)
    earlier = lax.broadcasted_iota(jnp.int32, (n, n), 0)
    later = lax.broadcasted_iota(jnp.int32, (n, n), 1)
    upto = jnp.where(earlier <= later, 1.0, 0.0).astype(BF16)
    count = mm(hot.astype(BF16), upto)
    position = jnp.sum(hot * count, axis=0, keepdims=True) - 1.0
    slot = jnp.where(position < capacity, idx_row.astype(F32) * stride + position, -1.0)
    return hot, slot


def pick(slot, firsts, rows):
    n = slot.shape[1]
    row = lax.broadcasted_iota(jnp.int32, (rows, n), 0)
    parts = [jnp.where((row + first).astype(F32) == slot, 1.0, 0.0) for first in firsts]
    return jnp.concatenate(parts, axis=0).astype(BF16)


def gate_of(x, wgt, hot):
    n_experts = hot.shape[0]
    logits = mm(x, wgt, CONTRACT_LAST)
    e = jnp.exp(logits - jnp.max(logits, axis=1, keepdims=True))
    prob = e / jnp.sum(e, axis=1, keepdims=True)
    eye = jnp.where(
        lax.broadcasted_iota(jnp.int32, (n_experts, n_experts), 0)
        == lax.broadcasted_iota(jnp.int32, (n_experts, n_experts), 1), 1.0, 0.0)
    chosen = mm(hot.astype(BF16), eye.astype(BF16), CONTRACT_FIRST)
    gate = jnp.sum(chosen * prob, axis=1, keepdims=True)
    return prob, chosen, gate


def enter(*devices):
    barrier = pltpu.get_barrier_semaphore()
    for device in devices:
        pl.semaphore_signal(barrier, inc=1, device_id=device, device_id_type=MESH)
    return barrier


def send(src, dst, ssem, rsem, device):
    copy = pltpu.make_async_remote_copy(
        src_ref=src, dst_ref=dst, send_sem=ssem, recv_sem=rsem, device_id=device, device_id_type=MESH)
    copy.start()
    return copy


def make_front(n_experts, capacity, cap):
    blk = 2 * cap

    def front(x_hbm, gy_hbm, wgt_hbm, idx_hbm, wi_hbm, wo_hbm,
              h_ref, da_ref, xs_ref, dys_ref, sfar_ref, snear_ref, sfar_own_ref, snear_own_ref, ynear_ref, yfar0_ref, yfar1_ref,
              picks_ref, prob_ref, chosen_ref,
              x_ref, gy_ref, wgt_ref, idx_ref, wi, wo, xsend, dysend, gp,
              ypeer, yown, yrecv, yback, yland,
              in_sem, wsem, x_s, x_r, d_s, d_r, y_s, y_r, b_s, b_r):
        tp = lax.axis_index("tp")
        tp_peer = 1 - tp
        peers = ep_partners()
        half = x_ref.shape[1] // 2
        mine = pl.ds(pl.multiple_of(tp * half, half), half)
        theirs = pl.ds(pl.multiple_of(tp_peer * half, half), half)
        d_ff = wi.shape[2]
        near, far, whole = slice(0, blk), slice(blk, 2 * blk), slice(0, 2 * blk)
        small = [pltpu.make_async_copy(src, dst, in_sem.at[k]) for k, (src, dst) in enumerate(
            ((idx_hbm, idx_ref), (x_hbm, x_ref), (wgt_hbm, wgt_ref), (gy_hbm, gy_ref)))]
        for copy in small:
            copy.start()
        barrier = enter({"ep": peers[1]}, {"ep": peers[2]}, {"ep": peers[3]}, {"tp": tp_peer})
        loads = {}
        for e in range(2):
            loads["i", e] = pltpu.make_async_copy(wi_hbm.at[e], wi.at[e], wsem.at[0, e])
            loads["o", e] = pltpu.make_async_copy(wo_hbm.at[e], wo.at[e], wsem.at[1, e])
        loads["i", 0].start()
        loads["o", 0].start()

        xc, dc, yc = {}, {}, {}

        def dispatch(v, g, e, buf, rows_ref, ssem, rsem, made):
            first = [peers[2 * g + q] * blk + e * cap for q in range(2)]
            rows = mm(pick(slot, first, cap), v)
            for q in range(2):
                r = 2 * g + q
                part = rows[q * cap:(q + 1) * cap].astype(BF16)
                if r == 0:
                    rows_ref[e, 0:cap, :] = part
                else:
                    buf[r - 1, e] = part
            return lambda: [made.__setitem__((r, e), send(
                buf.at[r - 1, e], rows_ref.at[e, r * cap:(r + 1) * cap, :], ssem.at[r - 1, e], rsem.at[r - 1, e],
                {"ep": peers[r]})) for r in (2 * g, 2 * g + 1) if r]

        def dispatch_x(g, e):
            return dispatch(x_ref[...], g, e, xsend, xs_ref, x_s, x_r, xc)

        small[0].wait()
        hot, slot = route(idx_ref[...], capacity, n_experts, cap)
        small[1].wait()
        go = dispatch_x(0, 0)
        pl.semaphore_wait(barrier, 4)
        go()
        dispatch_x(1, 0)()
        dispatch_x(0, 1)()
        dispatch_x(1, 1)()
        loads["i", 1].start()
        loads["o", 1].start()

        def forward(g, e):
            rows = far if g else near
            if g == 0:
                loads["i", e].wait()
            xg = xs_ref[e, rows, :]
            step = d_ff // 2
            for c in range(2):
                cols = slice(c * step, (c + 1) * step)
                a = mm(xg, wi[e, :, cols])
                t = jnp.tanh(GELU_C * (a + GELU_K * (a * a * a)))
                cdf = 0.5 * (1.0 + t)
                h_ref[e, rows, cols] = (a * cdf).astype(BF16)
                gp[e, rows, cols] = cdf + (0.5 * a) * (1.0 - t * t) * (GELU_C + (3.0 * GELU_C * GELU_K) * (a * a))
            if g == 0:
                loads["o", e].wait()
            ypeer[g, e] = mm(h_ref[e, rows, :], wo[e, :, theirs])
            yc[g, e] = send(ypeer.at[g, e], yrecv.at[g, e], y_s.at[g, e], y_r.at[g, e], {"tp": tp_peer})

        def backward(rows, e):
            dyg = dys_ref[e, rows, :]
            step = d_ff // 4
            for c in range(4):
                cols = slice(c * step, (c + 1) * step)
                dh = mm(dyg, wo[e, cols, :], CONTRACT_LAST)
                da_ref[e, rows, cols] = (dh * gp[e, rows, cols]).astype(BF16)
            dag = da_ref[e, rows, :]
            for cols, near_ref, far_ref in ((theirs, snear_ref, sfar_ref), (mine, snear_own_ref, sfar_own_ref)):
                part = mm(dag, wi[e, cols, :], CONTRACT_LAST)
                if rows is not far:
                    near_ref[e] = part[0:blk]
                if rows is not near:
                    far_ref[e] = part[part.shape[0] - blk:]

        def y_blocks(g):
            for e in range(2):
                yc[g, e].wait()
            both = [yown[e, far if g else near, :] + yrecv[g, e] for e in range(2)]
            return [jnp.concatenate([both[e][q * cap:(q + 1) * cap] for e in range(2)], axis=0).astype(BF16) for q in range(2)]

        xc[1, 0].wait()
        forward(0, 0)
        small[2].wait()
        small[3].wait()
        prob, chosen, gate = gate_of(x_ref[...], wgt_ref[...], hot)
        prob_ref[...], chosen_ref[...] = prob, chosen
        dy = (gate * gy_ref[...].astype(F32)).astype(BF16)
        for g in (1, 0):
            for e in range(2):
                dispatch(dy, g, e, dysend, dys_ref, d_s, d_r, dc)()
        xc[1, 1].wait()
        forward(0, 1)
        picks_ref[...] = pick(slot, [peers[r] * blk for r in range(4)], blk)
        xc[2, 0].wait()
        xc[3, 0].wait()
        forward(1, 0)
        dc[1, 0].wait()
        backward(near, 0)
        xc[2, 1].wait()
        xc[3, 1].wait()
        forward(1, 1)
        for e in range(2):
            yown[e] = mm(h_ref[e], wo[e, :, mine])
        kept, away = y_blocks(0)
        ynear_ref[near, :] = kept
        yback[...] = away
        bc = send(yback, yland, b_s, b_r, {"ep": peers[1]})
        dc[2, 0].wait()
        dc[3, 0].wait()
        backward(far, 0)
        for r in (1, 2, 3):
            dc[r, 1].wait()
        backward(whole, 1)
        bc.wait()
        ynear_ref[far, :] = yland[...]
        yfar0_ref[...], yfar1_ref[...] = y_blocks(1)

    return front


def make_grad(pieces, tell):
    def grad(left_ref, right_ref, after_ref, *rest):
        rest = rest[len(rest) - 3 - tell:]
        out_hbm, rest = rest[0], rest[1:]
        buf, sem = rest[-2:]
        size = buf.shape[1]
        copies = []
        for k, (e, row) in enumerate(pieces):
            rows = slice(row, row + size)
            buf[k] = mm(left_ref[e, :, rows], right_ref[e], CONTRACT_FIRST)
            copies.append(pltpu.make_async_copy(buf.at[k], out_hbm.at[e, rows, :], sem.at[k]))
            copies[-1].start()
        if tell:
            rest[0][...] = jnp.zeros_like(rest[0])
        for copy in copies:
            copy.wait()

    return grad


def y_tokens(picks_ref, ynear_ref, yfar0_ref, yfar1_ref, after_ref, y_ref):
    rows = jnp.concatenate([ynear_ref[...], yfar0_ref[...], yfar1_ref[...]], axis=0)
    y_ref[...] = mm(picks_ref[...], rows, CONTRACT_FIRST).astype(BF16)


def make_blocks(cap):
    def s_blocks(own_ref, recv_ref, after_ref, out_ref):
        both = [own_ref[e] + recv_ref[e] for e in range(2)]
        out_ref[...] = jnp.concatenate(
            [both[e][q * cap:(q + 1) * cap] for q in range(2) for e in range(2)], axis=0).astype(BF16)

    return s_blocks


def make_near_return(cap):
    blk = 2 * cap

    def near_return(picks_ref, sfar_ref, sown_ref, srecv_ref, after_ref, stok_ref, sback, sland, b_s, b_r):
        partner = {"ep": ep_partners()[1]}
        barrier = enter(partner)
        both = [sown_ref[e] + srecv_ref[e] for e in range(2)]
        kept, away = [jnp.concatenate([both[e][q * cap:(q + 1) * cap] for e in range(2)], axis=0).astype(BF16)
                      for q in range(2)]
        sback[...] = away
        pl.semaphore_wait(barrier, 1)
        copies = [send(sback, sland.at[0], b_s.at[0], b_r.at[0], partner),
                  send(sfar_ref.at[blk:2 * blk, :], sland.at[1], b_s.at[1], b_r.at[1], partner)]
        for copy in copies:
            copy.wait()
        s_rows = jnp.concatenate([kept, sland[0], sfar_ref[0:blk, :], sland[1]], axis=0)
        stok_ref[...] = mm(picks_ref[...], s_rows, CONTRACT_FIRST).astype(BF16)

    return near_return


def router_grad(x_ref, gy_ref, prob_ref, chosen_ref, ymine_ref, ytheirs_ref, after_ref, dlog_ref, dwgt_ref, dwg, w_s, w_r):
    tp = lax.axis_index("tp")
    ep = lax.axis_index("ep")
    peers = ep_partners()
    half = ymine_ref.shape[1]
    barrier = enter(*[{"ep": peers[r]} for r in (1, 2, 3)])
    sums = [jnp.sum(gy_ref[:, pl.ds(pl.multiple_of(side * half, half), half)].astype(F32) * ref[...].astype(F32),
                    axis=1, keepdims=True) for side, ref in ((tp, ymine_ref), (1 - tp, ytheirs_ref))]
    prob, chosen = prob_ref[...], chosen_ref[...]
    gate = jnp.sum(chosen * prob, axis=1, keepdims=True)
    dlogits = ((sums[0] + sums[1]) * prob * (chosen - gate)).astype(BF16)
    dlog_ref[...] = dlogits
    dwg[ep] = mm(dlogits, x_ref[...], CONTRACT_FIRST)
    pl.semaphore_wait(barrier, 3)
    copies = [send(dwg.at[ep], dwg.at[ep], w_s.at[r - 1], w_r.at[r - 1], {"ep": peers[r]}) for r in (2, 3, 1)]
    for copy in copies:
        copy.wait()
    dwgt_ref[...] = (dwg[0] + dwg[1]) + (dwg[2] + dwg[3])


def write_out(dwgt_ref, ymine_ref, ytheirs_ref, prob_ref, chosen_ref, out_hbm, dwgt_hbm, out_ref, sem):
    half = ymine_ref.shape[1]
    first = pltpu.make_async_copy(dwgt_ref, dwgt_hbm, sem.at[0])
    first.start()
    tp = lax.axis_index("tp")
    gate = jnp.sum(chosen_ref[...] * prob_ref[...], axis=1, keepdims=True)
    for side, ref in ((tp, ymine_ref), (1 - tp, ytheirs_ref)):
        out_ref[:, pl.ds(pl.multiple_of(side * half, half), half)] = (gate * ref[...].astype(F32)).astype(BF16)
    second = pltpu.make_async_copy(out_ref, out_hbm, sem.at[1])
    second.start()
    first.wait()
    second.wait()


def write_dx(dlog_ref, wgt_ref, smine_ref, stheirs_ref, after_ref, dx_hbm, dx_ref, sem):
    half = smine_ref.shape[1]
    tp = lax.axis_index("tp")
    for side, ref in ((tp, smine_ref), (1 - tp, stheirs_ref)):
        cols = pl.ds(pl.multiple_of(side * half, half), half)
        dx_ref[:, cols] = (ref[...].astype(F32) + mm(dlog_ref[...], wgt_ref[:, cols])).astype(BF16)
    copy = pltpu.make_async_copy(dx_ref, dx_hbm, sem)
    copy.start()
    copy.wait()


FIRST_PART = 12


def solution(mesh):
    row_spec = P(("dp", "ep"), None)
    vmem = pl.BlockSpec(memory_space=pltpu.VMEM)
    hbm = pl.BlockSpec(memory_space=pltpu.HBM)

    def local_block(tokens, grad_out, w_router, w_in, w_out, expert_ids):
        n, d_model = tokens.shape
        n_experts = w_router.shape[1]
        le, _, d_ff = w_in.shape
        capacity = (6 * n + 5 * n_experts - 1) // (5 * n_experts)
        cap = -(-capacity // 8) * 8
        blk = le * cap
        rows = 4 * cap
        half = d_model // 2
        wgt = w_router.T
        idx_row = expert_ids.reshape(1, n)
        sds = jax.ShapeDtypeStruct
        dma = pltpu.SemaphoreType.DMA

        h, da, xs, dys, sfar, snear, sfar_own, snear_own, ynear, yfar0, yfar1, picks, prob, chosen = pl.pallas_call(
            make_front(n_experts, capacity, cap),
            out_shape=(sds((le, rows, d_ff), BF16), sds((le, rows, d_ff), BF16), sds((le, rows, d_model), BF16),
                       sds((le, rows, d_model), BF16), *[sds((le, blk, half), F32)] * 4,
                       sds((2 * blk, half), BF16), sds((blk, half), BF16), sds((blk, half), BF16),
                       sds((4 * blk, n), BF16), sds((n, n_experts), F32), sds((n, n_experts), F32)),
            in_specs=[hbm] * 6,
            out_specs=(vmem,) * 14,
            scratch_shapes=[
                pltpu.VMEM((n, d_model), BF16), pltpu.VMEM((n, d_model), BF16), pltpu.VMEM((n_experts, d_model), BF16),
                pltpu.VMEM((1, n), jnp.int32),
                pltpu.VMEM((le, d_model, d_ff), BF16), pltpu.VMEM((le, d_ff, d_model), BF16),
                pltpu.VMEM((3, le, cap, d_model), BF16), pltpu.VMEM((3, le, cap, d_model), BF16),
                pltpu.VMEM((le, rows, d_ff), F32),
                pltpu.VMEM((2, le, blk, half), F32), pltpu.VMEM((le, rows, half), F32), pltpu.VMEM((2, le, blk, half), F32),
                pltpu.VMEM((blk, half), BF16), pltpu.VMEM((blk, half), BF16),
                dma((4,)), dma((2, le)), dma((3, le)), dma((3, le)), dma((3, le)), dma((3, le)), dma((2, le)), dma((2, le)), dma, dma,
            ],
            compiler_params=pltpu.CompilerParams(collective_id=0, has_side_effects=True, vmem_limit_bytes=40 * 2**20),
            name="front",
        )(*[pltpu.with_memory_space_constraint(v, pltpu.HBM) for v in (tokens, grad_out, wgt, idx_row, w_in, w_out)])

        swap = [(0, 1), (1, 0)]
        across, diagonal = [(0, 2), (2, 0), (1, 3), (3, 1)], [(0, 3), (3, 0), (1, 2), (2, 1)]
        sfar_recv = lax.ppermute(sfar, "tp", swap)
        snear_recv = lax.ppermute(snear, "tp", swap)
        yland0 = lax.ppermute(yfar0, "ep", across)
        yland1 = lax.ppermute(yfar1, "ep", diagonal)

        def local(kernel, out_shape, ins, outs, args, scratch=(), limit=8, **more):
            return pl.pallas_call(
                kernel, out_shape=out_shape, in_specs=ins, out_specs=outs, scratch_shapes=list(scratch),
                compiler_params=pltpu.CompilerParams(vmem_limit_bytes=limit * 2**20), **more)(*args)

        def weight_grad(left, right, after, pieces, size, tell, base=None):
            shape = (le, left.shape[2], right.shape[2])
            cost = pl.CostEstimate(flops=2 * rows * len(pieces) * size * shape[2],
                                   bytes_accessed=4 * len(pieces) * size * shape[2], transcendentals=0)
            return local(
                make_grad(pieces, tell), (sds(shape, F32), sds((8, 128), F32))[:1 + tell],
                [vmem] * 3 + [hbm] * (base is not None), (hbm, vmem)[:1 + tell],
                (left, right, after) + ((base,) if base is not None else ()),
                [pltpu.VMEM((len(pieces), size, shape[2]), F32), dma((len(pieces),))], 24, cost_estimate=cost,
                input_output_aliases={3: 0} if base is not None else {})

        out_size, in_size = d_ff // 8, d_model // 8
        out_pieces = [(e, c * out_size) for e in range(le) for c in range(8)]
        in_pieces = [(e, c * in_size) for e in range(le) for c in range(8)]
        dwo, done = weight_grad(h, dys, ynear, out_pieces, out_size, True)
        ymine = local(y_tokens, sds((n, half), BF16), [vmem] * 5, vmem, (picks, ynear, yland0, yland1, done))
        ytheirs = lax.ppermute(ymine, "tp", swap)
        sblocks = local(make_blocks(cap), sds((2 * blk, half), BF16), [vmem] * 3, vmem, (sfar_own, sfar_recv, ymine))
        sfar_land = lax.ppermute(sblocks, "ep", across)
        dwi, done = weight_grad(xs, da, sblocks, in_pieces[:FIRST_PART], in_size, True)

        smine = pl.pallas_call(
            make_near_return(cap), out_shape=sds((n, half), BF16), in_specs=[vmem] * 5, out_specs=vmem,
            scratch_shapes=[pltpu.VMEM((blk, half), BF16), pltpu.VMEM((2, blk, half), BF16), dma((2,)), dma((2,))],
            compiler_params=pltpu.CompilerParams(collective_id=1, has_side_effects=True, vmem_limit_bytes=8 * 2**20),
            name="near_return",
        )(picks, sfar_land, snear_own, snear_recv, done)
        stheirs = lax.ppermute(smine, "tp", swap)
        dwi, done = weight_grad(xs, da, smine, in_pieces[FIRST_PART:], in_size, True, dwi)
        dlog, dwgt_v = pl.pallas_call(
            router_grad, out_shape=(sds((n, n_experts), BF16), sds((n_experts, d_model), F32)),
            in_specs=[vmem] * 7, out_specs=(vmem,) * 2,
            scratch_shapes=[pltpu.VMEM((4, n_experts, d_model), F32), dma((3,)), dma((3,))],
            compiler_params=pltpu.CompilerParams(collective_id=2, has_side_effects=True, vmem_limit_bytes=8 * 2**20),
            name="router_grad",
        )(tokens, grad_out, prob, chosen, ymine, ytheirs, done)
        out, dwgt = local(write_out, (sds((n, d_model), BF16), sds((n_experts, d_model), F32)), [vmem] * 5, (hbm,) * 2,
                          (dwgt_v, ymine, ytheirs, prob, chosen), [pltpu.VMEM((n, d_model), BF16), dma((2,))])
        dx = local(write_dx, sds((n, d_model), BF16), [vmem] * 5, hbm, (dlog, wgt, smine, stheirs, dwgt_v),
                   [pltpu.VMEM((n, d_model), BF16), dma])
        return out, dx, dwi, dwo, dwgt.T

    in_specs = (row_spec, row_spec, P(None, None), P("ep", None, "tp"), P("ep", "tp", None), P(("dp", "ep")))
    out_specs = (row_spec, row_spec, P(("dp", "ep"), None, "tp"), P(("dp", "ep"), "tp", None), P("dp", None))
    return jax.shard_map(local_block, mesh=mesh, in_specs=in_specs, out_specs=out_specs, check_vma=False)
```

profile of v0, /device:TPU:0, one launch (start us, length us, event | category | flops | bytes accessed | tf_op | source)
XLA Modules:
  0.0 53.3 jit_solution(2902700704243344117)
XLA Ops:
  0.6 23.1 %front.1 = (bf16[2,160,2048]{2,1,0:T(8,128)(2,1)S(1)}, bf16[2,160,2048]{2,1,0:T(8,128)(2,1)S(1)}, bf16[2,160,1024]{2,1,0:T(8,128)(2,1)S(1)}, bf16[2,160,1024]{2,...) custom-call(bf16[256,1024]{1,0:T(8,128)(2,1)} %x_ref.1, ...), custom_call_target="tpu_custom_call" | custom-call | tf_op jit(solution)/shard_map/front/pallas_call | solution.py:335
  23.7 0.6 %collective-permute-start.3 = (f32[2,80,512]{2,1,0:T(8,128)S(1)}, f32[2,80,512]{2,1,0:T(8,128)S(1)}, u32[]{:S(2)}, u32[]{:S(2)}) collective-permute-start(f32[2,80,512]{2,1,0:T(8,128)S(1)} %get-tuple-element.41), channel_id=1, source_target_pairs={{0,4},{4,0},{1,5},{5,1},{2,6},{6,2},{3,7},{7,3}} | collective-permute-start | bytes 983048 | tf_op jit(solution)/shard_map/ppermute | solution.py:359
  24.3 1.5 %collective-permute-start.5 = (f32[2,80,512]{2,1,0:T(8,128)S(1)}, f32[2,80,512]{2,1,0:T(8,128)S(1)}, u32[]{:S(2)}, u32[]{:S(2)}) collective-permute-start(f32[2,80,512]{2,1,0:T(8,128)S(1)} %get-tuple-element.43), channel_id=1, source_target_pairs={{0,4},{4,0},{1,5},{5,1},{2,6},{6,2},{3,7},{7,3}} | collective-permute-start | bytes 983048 | tf_op jit(solution)/shard_map/ppermute | solution.py:360
  25.8 1.3 %collective-permute-start = (bf16[80,512]{1,0:T(8,128)(2,1)S(1)}, bf16[80,512]{1,0:T(8,128)(2,1)S(1)}, u32[]{:S(2)}, u32[]{:S(2)}) collective-permute-start(bf16[80,512]{1,0:T(8,128)(2,1)S(1)} %get-tuple-element.33), channel_id=1, source_target_pairs={{0,2},{2,0},{1,3},{3,1},{4,6},{6,4},{5,7},{7,5}} | collective-permute-start | bytes 245768 | tf_op jit(solution)/shard_map/ppermute | solution.py:361
  27.0 0.0 collective-permute-start.1
  27.0 6.3 %shard_map.101 = (f32[2,2048,1024]{2,1,0:T(8,128)}, f32[8,128]{1,0:T(8,128)S(1)}) custom-call(bf16[2,160,2048]{2,1,0:T(8,128)(2,1)S(1)} %get-tuple-element.35.left_ref, bf16[2,160,1024]{2,1,0:T(8,128)(2,1)S(1)} %get-tuple-element.36.right_ref, bf16[160,512]{1,0:T(8,128)(2,1)S(1)} %get-tuple-element.32.after_ref.ynear_ref), custom_call_target="tpu_custom_call" | custom-call | flops 1342177280 | bytes 16777216 | tf_op jit(solution)/shard_map/pallas_call | solution.py:365
  33.3 0.0 collective-permute-done.yfar0_ref
  33.3 0.0 collective-permute-done.1.yfar1_ref
  33.3 0.3 shard_map.102.after_ref.ymine_ref
  33.7 0.7 %collective-permute-done.3.recv_ref = f32[2,80,512]{2,1,0:T(8,128)S(1)} collective-permute-done((f32[2,80,512]{2,1,0:T(8,128)S(1)}, f32[2,80,512]{2,1,0:T(8,128)S(1)}, u32[]{:S(2)}, u32[]{:S(2)}) %collective-permute-start.3) | collective-permute-done | bytes 327712 | tf_op jit(solution)/shard_map/ppermute | solution.py:359
  34.4 1.3 %collective-permute-start.4 = (bf16[160,512]{1,0:T(8,128)(2,1)S(1)}, bf16[160,512]{1,0:T(8,128)(2,1)S(1)}, u32[]{:S(2)}, u32[]{:S(2)}) collective-permute-start(bf16[160,512]{1,0:T(8,128)(2,1)S(1)} %shard_map.103.after_ref), channel_id=1, source_target_pairs={{0,2},{2,0},{1,3},{3,1},{4,6},{6,4},{5,7},{7,5}} | collective-permute-start | bytes 491528 | tf_op jit(solution)/shard_map/ppermute | solution.py:387
  35.6 0.8 %collective-permute-start.2 = (bf16[256,512]{1,0:T(8,128)(2,1)S(1)}, bf16[256,512]{1,0:T(8,128)(2,1)S(1)}, u32[]{:S(2)}, u32[]{:S(2)}) collective-permute-start(bf16[256,512]{1,0:T(8,128)(2,1)S(1)} %shard_map.102.after_ref.ymine_ref), channel_id=1, source_target_pairs={{0,4},{4,0},{1,5},{5,1},{2,6},{6,2},{3,7},{7,3}} | collective-permute-start | bytes 786440 | tf_op jit(solution)/shard_map/ppermute | solution.py:385
  36.4 5.0 %shard_map.104 = (f32[2,1024,2048]{2,1,0:T(8,128)}, f32[8,128]{1,0:T(8,128)S(1)}) custom-call(bf16[2,160,1024]{2,1,0:T(8,128)(2,1)S(1)} %get-tuple-element.38.left_ref, bf16[2,160,2048]{2,1,0:T(8,128)(2,1)S(1)} %get-tuple-element.39.right_ref, bf16[160,512]{1,0:T(8,128)(2,1)S(1)} %shard_map.103.after_ref), custom_call_target="tpu_custom_call" | custom-call | flops 1006632960 | bytes 12582912 | tf_op jit(solution)/shard_map/pallas_call | solution.py:365
  41.4 0.0 collective-permute-done.5.srecv_ref
  41.4 0.0 collective-permute-done.4.sfar_ref
  41.4 1.8 %near_return.1.after_ref.smine_ref = bf16[256,512]{1,0:T(8,128)(2,1)S(1)} custom-call(bf16[320,256]{1,0:T(8,128)(2,1)S(1)} %get-tuple-element.31.picks_ref, bf16[160,512]{1,0:T(8,128)(2,1)S(1)} %collective-permute-done.4.sfar_ref, f32[2,80,512]{2,1,0:T(8,128)S(1)} %get-tuple-element.42.sown_ref, f32[2,80,512]{2,1,0:T(8,128)S(1)} %collective-permute-done.5.srecv_ref, ...), custom_call_target="tpu_custom_call" | custom-call | tf_op jit(solution)/shard_map/near_return/pallas_call | solution.py:390
  43.2 1.3 %collective-permute-start.6 = (bf16[256,512]{1,0:T(8,128)(2,1)S(1)}, bf16[256,512]{1,0:T(8,128)(2,1)S(1)}, u32[]{:S(2)}, u32[]{:S(2)}) collective-permute-start(bf16[256,512]{1,0:T(8,128)(2,1)S(1)} %near_return.1.after_ref.smine_ref), channel_id=1, source_target_pairs={{0,4},{4,0},{1,5},{5,1},{2,6},{6,2},{3,7},{7,3}} | collective-permute-start | bytes 786440 | tf_op jit(solution)/shard_map/ppermute | solution.py:396
  44.5 0.0 copy-start
  44.5 0.0 copy-start.1
  44.5 0.0 copy-start.2
  44.5 2.4 %shard_map.105 = (f32[2,1024,2048]{2,1,0:T(8,128)}, f32[8,128]{1,0:T(8,128)S(1)}) custom-call(bf16[2,160,1024]{2,1,0:T(8,128)(2,1)S(1)} %get-tuple-element.38.left_ref, bf16[2,160,2048]{2,1,0:T(8,128)(2,1)S(1)} %get-tuple-element.39.right_ref, bf16[256,512]{1,0:T(8,128)(2,1)S(1)} %near_return.1.after_ref.smine_ref, ...), custom_call_target="tpu_custom_call", output_to_operand_aliasing={{0}: (3, {})} | custom-call | flops 335544320 | bytes 4194304 | tf_op jit(solution)/shard_map/pallas_call | solution.py:365
  46.8 0.0 collective-permute-done.2.ytheirs_ref
  46.9 0.0 copy-done
  46.9 0.0 copy-done.1
  46.9 4.1 %router_grad.1 = (bf16[256,8]{1,0:T(8,128)(2,1)S(1)}, f32[8,1024]{1,0:T(8,128)S(1)}) custom-call(bf16[256,1024]{1,0:T(8,128)(2,1)S(1)} %copy-done, bf16[256,1024]{1,0:T(8,128)(2,1)S(1)} %copy-done.1, f32[256,8]{1,0:T(8,128)S(1)} %get-tuple-element.29.prob_ref, f32[256,8]{1,0:T(8,128)S(1)} %get-tuple-element.30.chosen_ref, ...), custom_call_target="tpu_custom_call" | custom-call | tf_op jit(solution)/shard_map/router_grad/pallas_call | solution.py:398
  51.0 1.0 %shard_map.106 = (bf16[256,1024]{1,0:T(8,128)(2,1)}, f32[8,1024]{1,0:T(8,128)}) custom-call(f32[8,1024]{1,0:T(8,128)S(1)} %get-tuple-element.47.dwgt_ref.after_ref, bf16[256,512]{1,0:T(8,128)(2,1)S(1)} %shard_map.102.after_ref.ymine_ref, bf16[256,512]{1,0:T(8,128)(2,1)S(1)} %collective-permute-done.2.ytheirs_ref, f32[256,8]{1,0:T(8,128)S(1)} %get-tuple-element.29.prob_ref, ...), custom_call_target="tpu_custom_call" | custom-call | tf_op jit(solution)/shard_map/pallas_call | solution.py:365
  52.0 0.0 collective-permute-done.6.stheirs_ref
  52.0 0.0 copy-done.2
  52.0 1.1 %shard_map.107 = bf16[256,1024]{1,0:T(8,128)(2,1)} custom-call(bf16[256,8]{1,0:T(8,128)(2,1)S(1)} %get-tuple-element.49.dlog_ref, bf16[8,1024]{1,0:T(8,128)(2,1)S(1)} %bitcast.4, bf16[256,512]{1,0:T(8,128)(2,1)S(1)} %near_return.1.after_ref.smine_ref, bf16[256,512]{1,0:T(8,128)(2,1)S(1)} %collective-permute-done.6.stheirs_ref, ...), custom_call_target="tpu_custom_call" | custom-call | tf_op jit(solution)/shard_map/pallas_call | solution.py:365
  (1 shorter events, 0.0 us)
Async XLA Ops:
  23.7 10.6 %collective-permute-start.3 = (f32[2,80,512]{2,1,0:T(8,128)S(1)}, f32[2,80,512]{2,1,0:T(8,128)S(1)}, u32[]{:S(2)}, u32[]{:S(2)}) collective-permute-start(f32[2,80,512]{2,1,0:T(8,128)S(1)} %get-tuple-element.41), channel_id=1, source_target_pairs={{0,4},{4,0},{1,5},{5,1},{2,6},{6,2},{3,7},{7,3}} | collective-permute-start | bytes 983048 | tf_op jit(solution)/shard_map/ppermute | solution.py:359
  24.3 17.1 %collective-permute-start.5 = (f32[2,80,512]{2,1,0:T(8,128)S(1)}, f32[2,80,512]{2,1,0:T(8,128)S(1)}, u32[]{:S(2)}, u32[]{:S(2)}) collective-permute-start(f32[2,80,512]{2,1,0:T(8,128)S(1)} %get-tuple-element.43), channel_id=1, source_target_pairs={{0,4},{4,0},{1,5},{5,1},{2,6},{6,2},{3,7},{7,3}} | collective-permute-start | bytes 983048 | tf_op jit(solution)/shard_map/ppermute | solution.py:360
  25.8 7.6 %collective-permute-start = (bf16[80,512]{1,0:T(8,128)(2,1)S(1)}, bf16[80,512]{1,0:T(8,128)(2,1)S(1)}, u32[]{:S(2)}, u32[]{:S(2)}) collective-permute-start(bf16[80,512]{1,0:T(8,128)(2,1)S(1)} %get-tuple-element.33), channel_id=1, source_target_pairs={{0,2},{2,0},{1,3},{3,1},{4,6},{6,4},{5,7},{7,5}} | collective-permute-start | bytes 245768 | tf_op jit(solution)/shard_map/ppermute | solution.py:361
  27.0 6.3 %collective-permute-start.1 = (bf16[80,512]{1,0:T(8,128)(2,1)S(1)}, bf16[80,512]{1,0:T(8,128)(2,1)S(1)}, u32[]{:S(2)}, u32[]{:S(2)}) collective-permute-start(bf16[80,512]{1,0:T(8,128)(2,1)S(1)} %get-tuple-element.34), channel_id=1, source_target_pairs={{0,3},{3,0},{1,2},{2,1},{4,7},{7,4},{5,6},{6,5}} | collective-permute-start | bytes 245768 | tf_op jit(solution)/shard_map/ppermute | solution.py:362
  34.4 7.1 %collective-permute-start.4 = (bf16[160,512]{1,0:T(8,128)(2,1)S(1)}, bf16[160,512]{1,0:T(8,128)(2,1)S(1)}, u32[]{:S(2)}, u32[]{:S(2)}) collective-permute-start(bf16[160,512]{1,0:T(8,128)(2,1)S(1)} %shard_map.103.after_ref), channel_id=1, source_target_pairs={{0,2},{2,0},{1,3},{3,1},{4,6},{6,4},{5,7},{7,5}} | collective-permute-start | bytes 491528 | tf_op jit(solution)/shard_map/ppermute | solution.py:387
  35.6 11.2 %collective-permute-start.2 = (bf16[256,512]{1,0:T(8,128)(2,1)S(1)}, bf16[256,512]{1,0:T(8,128)(2,1)S(1)}, u32[]{:S(2)}, u32[]{:S(2)}) collective-permute-start(bf16[256,512]{1,0:T(8,128)(2,1)S(1)} %shard_map.102.after_ref.ymine_ref), channel_id=1, source_target_pairs={{0,4},{4,0},{1,5},{5,1},{2,6},{6,2},{3,7},{7,3}} | collective-permute-start | bytes 786440 | tf_op jit(solution)/shard_map/ppermute | solution.py:385
  43.2 8.8 %collective-permute-start.6 = (bf16[256,512]{1,0:T(8,128)(2,1)S(1)}, bf16[256,512]{1,0:T(8,128)(2,1)S(1)}, u32[]{:S(2)}, u32[]{:S(2)}) collective-permute-start(bf16[256,512]{1,0:T(8,128)(2,1)S(1)} %near_return.1.after_ref.smine_ref), channel_id=1, source_target_pairs={{0,4},{4,0},{1,5},{5,1},{2,6},{6,2},{3,7},{7,3}} | collective-permute-start | bytes 786440 | tf_op jit(solution)/shard_map/ppermute | solution.py:396
  44.5 2.4 %copy-start = (bf16[256,1024]{1,0:T(8,128)(2,1)S(1)}, bf16[256,1024]{1,0:T(8,128)(2,1)}, u32[]{:S(2)}) copy-start(bf16[256,1024]{1,0:T(8,128)(2,1)} %x_ref.1) | copy-start | bytes 1572868
  44.5 2.4 %copy-start.1 = (bf16[256,1024]{1,0:T(8,128)(2,1)S(1)}, bf16[256,1024]{1,0:T(8,128)(2,1)}, u32[]{:S(2)}) copy-start(bf16[256,1024]{1,0:T(8,128)(2,1)} %gy_ref.1) | copy-start | bytes 1572868
  44.5 7.5 %copy-start.2 = (bf16[1024,8]{0,1:T(8,128)(2,1)S(1)}, bf16[1024,8]{0,1:T(8,128)(2,1)}, u32[]{:S(2)}) copy-start(bf16[1024,8]{0,1:T(8,128)(2,1)} %param.8) | copy-start | bytes 49156
where the time goes:
time: 53.4 us; the launch traced here: 53.3 us
  Pallas kernels  45 us (84%)
  starting transfers between devices  6.62 us (12%)
  between operations  0.94 us (2%)
  waiting for transfers between devices  0.67 us (1%)
    pallas_call x1, Pallas kernels, local_block(): pl.pallas_call(make_front(n_experts, capacity, cap), out_shape=(sds((le,...  23.1 us
    pallas_call x7, Pallas kernels, local(): pl.pallas_call(kernel, out_shape=out_shape, in_specs=ins, out_specs=outs,...  16 us
    pallas_call x1, Pallas kernels, local_block(): pl.pallas_call(router_grad, out_shape=(sds((n, n_experts), BF16), sds((n_...  4.14 us
    pallas_call x1, Pallas kernels, local_block(): pl.pallas_call(make_near_return(cap), out_shape=sds((n, half), BF16), in_...  1.77 us
    ppermute x1, starting transfers between devices, local_block(): snear_recv = lax.ppermute(snear, 'tp', swap)  1.48 us
    ppermute x1, starting transfers between devices, local_block(): sfar_land = lax.ppermute(sblocks, 'ep', across)  1.27 us
    ppermute x1, starting transfers between devices, local_block(): stheirs = lax.ppermute(smine, 'tp', swap)  1.26 us
    ppermute x1, starting transfers between devices, local_block(): yland0 = lax.ppermute(yfar0, 'ep', across)  1.25 us
  transfers between devices with their start and end apart: 7, of which 1 were waited for; matrix products, arithmetic and copies ran while one was open for 0% of the time, Pallas kernels for 39%

commit v1 on v0

--- a/solution.py
+++ b/solution.py
@@ -75,9 +75,9 @@
     blk = 2 * cap
 
     def front(x_hbm, gy_hbm, wgt_hbm, idx_hbm, wi_hbm, wo_hbm,
-              h_ref, da_ref, xs_ref, dys_ref, sfar_ref, snear_ref, sfar_own_ref, snear_own_ref, ynear_ref, yfar0_ref, yfar1_ref,
-              picks_ref, prob_ref, chosen_ref,
-              x_ref, gy_ref, wgt_ref, idx_ref, wi, wo, xsend, dysend, gp,
+              h_ref, da_ref, xs_ref, dys_ref, sfar_ref, snear_ref, ynear_ref, yfar0_ref, yfar1_ref,
+              picks_ref, prob_ref, chosen_ref, wi,
+              x_ref, gy_ref, wgt_ref, idx_ref, wo, xsend, dysend, gp,
               ypeer, yown, yrecv, yback, yland,
               in_sem, wsem, x_s, x_r, d_s, d_r, y_s, y_r, b_s, b_r):
         tp = lax.axis_index("tp")
@@ -96,9 +96,9 @@
         loads = {}
         for e in range(2):
             loads["i", e] = pltpu.make_async_copy(wi_hbm.at[e], wi.at[e], wsem.at[0, e])
-            loads["o", e] = pltpu.make_async_copy(wo_hbm.at[e], wo.at[e], wsem.at[1, e])
+            for k, (name, cols) in enumerate((("theirs", theirs), ("mine", mine))):
+                loads[name, e] = pltpu.make_async_copy(wo_hbm.at[e, :, cols], wo.at[e, :, cols], wsem.at[1 + k, e])
         loads["i", 0].start()
-        loads["o", 0].start()
 
         xc, dc, yc = {}, {}, {}
 
@@ -113,27 +113,19 @@
                 else:
                     buf[r - 1, e] = part
             return lambda: [made.__setitem__((r, e), send(
-                buf.at[r - 1, e], rows_ref.at[e, r * cap:(r + 1) * cap, :], ssem.at[r - 1, e], rsem.at[r - 1, e],
+                buf.at[r - 1, e], rows_ref.at[e, r * cap:(r + 1) * cap, :], ssem, rsem.at[g, e],
                 {"ep": peers[r]})) for r in (2 * g, 2 * g + 1) if r]
+
+        def arrived(g, e, rows_ref, rsem):
+            part = rows_ref.at[e, far if g else slice(cap, blk), :]
+            pltpu.make_async_copy(part, part, rsem.at[g, e]).wait()
 
         def dispatch_x(g, e):
             return dispatch(x_ref[...], g, e, xsend, xs_ref, x_s, x_r, xc)
 
-        small[0].wait()
-        hot, slot = route(idx_ref[...], capacity, n_experts, cap)
-        small[1].wait()
-        go = dispatch_x(0, 0)
-        pl.semaphore_wait(barrier, 4)
-        go()
-        dispatch_x(1, 0)()
-        dispatch_x(0, 1)()
-        dispatch_x(1, 1)()
-        loads["i", 1].start()
-        loads["o", 1].start()
-
-        def forward(g, e):
-            rows = far if g else near
-            if g == 0:
+        def forward(first, last, e):
+            rows = slice(first * cap, last * cap)
+            if first == 0:
                 loads["i", e].wait()
             xg = xs_ref[e, rows, :]
             step = d_ff // 2
@@ -144,10 +136,23 @@
                 cdf = 0.5 * (1.0 + t)
                 h_ref[e, rows, cols] = (a * cdf).astype(BF16)
                 gp[e, rows, cols] = cdf + (0.5 * a) * (1.0 - t * t) * (GELU_C + (3.0 * GELU_C * GELU_K) * (a * a))
-            if g == 0:
-                loads["o", e].wait()
-            ypeer[g, e] = mm(h_ref[e, rows, :], wo[e, :, theirs])
-            yc[g, e] = send(ypeer.at[g, e], yrecv.at[g, e], y_s.at[g, e], y_r.at[g, e], {"tp": tp_peer})
+            if first == 0:
+                loads["theirs", e].wait()
+            ypeer[e, rows, :] = mm(h_ref[e, rows, :], wo[e, :, theirs])
+            yc[e, first] = send(ypeer.at[e, rows, :], yrecv.at[e, rows, :], y_s.at[e, first], y_r.at[e, first], {"tp": tp_peer})
+
+        small[0].wait()
+        hot, slot = route(idx_ref[...], capacity, n_experts, cap)
+        small[1].wait()
+        go = dispatch_x(0, 0)
+        loads["theirs", 0].start()
+        pl.semaphore_wait(barrier, 4)
+        go()
+        dispatch_x(1, 0)()
+        dispatch_x(0, 1)()
+        dispatch_x(1, 1)()
+        for copy in (loads["i", 1], loads["theirs", 1], loads["mine", 0], loads["mine", 1]):
+            copy.start()
 
         def backward(rows, e):
             dyg = dys_ref[e, rows, :]
@@ -157,21 +162,23 @@
                 dh = mm(dyg, wo[e, cols, :], CONTRACT_LAST)
                 da_ref[e, rows, cols] = (dh * gp[e, rows, cols]).astype(BF16)
             dag = da_ref[e, rows, :]
-            for cols, near_ref, far_ref in ((theirs, snear_ref, sfar_ref), (mine, snear_own_ref, sfar_own_ref)):
-                part = mm(dag, wi[e, cols, :], CONTRACT_LAST)
-                if rows is not far:
-                    near_ref[e] = part[0:blk]
-                if rows is not near:
-                    far_ref[e] = part[part.shape[0] - blk:]
+            part = mm(dag, wi[e, theirs, :], CONTRACT_LAST)
+            if rows is not far:
+                snear_ref[e] = part[0:blk]
+            if rows is not near:
+                sfar_ref[e] = part[part.shape[0] - blk:]
 
         def y_blocks(g):
+            rows = far if g else near
             for e in range(2):
-                yc[g, e].wait()
-            both = [yown[e, far if g else near, :] + yrecv[g, e] for e in range(2)]
+                for r in (2 * g, 2 * g + 1):
+                    if (e, r) in yc:
+                        yc[e, r].wait()
+            both = [yown[e, rows, :] + yrecv[e, rows, :] for e in range(2)]
             return [jnp.concatenate([both[e][q * cap:(q + 1) * cap] for e in range(2)], axis=0).astype(BF16) for q in range(2)]
 
-        xc[1, 0].wait()
-        forward(0, 0)
+        arrived(0, 0, xs_ref, x_r)
+        forward(0, 2, 0)
         small[2].wait()
         small[3].wait()
         prob, chosen, gate = gate_of(x_ref[...], wgt_ref[...], hot)
@@ -180,32 +187,33 @@
         for g in (1, 0):
             for e in range(2):
                 dispatch(dy, g, e, dysend, dys_ref, d_s, d_r, dc)()
-        xc[1, 1].wait()
-        forward(0, 1)
+        arrived(0, 1, xs_ref, x_r)
+        forward(0, 2, 1)
         picks_ref[...] = pick(slot, [peers[r] * blk for r in range(4)], blk)
-        xc[2, 0].wait()
-        xc[3, 0].wait()
-        forward(1, 0)
-        dc[1, 0].wait()
+        arrived(1, 0, xs_ref, x_r)
+        forward(2, 4, 0)
+        arrived(0, 0, dys_ref, d_r)
+        loads["mine", 0].wait()
         backward(near, 0)
-        xc[2, 1].wait()
-        xc[3, 1].wait()
-        forward(1, 1)
+        arrived(1, 1, xs_ref, x_r)
+        forward(2, 4, 1)
+        loads["mine", 1].wait()
         for e in range(2):
             yown[e] = mm(h_ref[e], wo[e, :, mine])
         kept, away = y_blocks(0)
         ynear_ref[near, :] = kept
         yback[...] = away
         bc = send(yback, yland, b_s, b_r, {"ep": peers[1]})
-        dc[2, 0].wait()
-        dc[3, 0].wait()
+        arrived(1, 0, dys_ref, d_r)
         backward(far, 0)
-        for r in (1, 2, 3):
-            dc[r, 1].wait()
+        for g in range(2):
+            arrived(g, 1, dys_ref, d_r)
         backward(whole, 1)
         bc.wait()
         ynear_ref[far, :] = yland[...]
         yfar0_ref[...], yfar1_ref[...] = y_blocks(1)
+        for sent, sem in ((xsend, x_s), (dysend, d_s)):
+            pltpu.make_async_copy(sent, sent, sem).wait()
 
     return front
 
@@ -228,6 +236,27 @@
             copy.wait()
 
     return grad
+
+
+def make_grad_out(pieces):
+    def grad_out(h_ref, dys_ref, da_ref, wi_ref, dwo_hbm, sfar_ref, snear_ref, buf, sem):
+        size = buf.shape[1]
+        blk, half = sfar_ref.shape[1:]
+        copies = []
+        for k, (e, row) in enumerate(pieces):
+            rows = slice(row, row + size)
+            buf[k] = mm(h_ref[e, :, rows], dys_ref[e], CONTRACT_FIRST)
+            copies.append(pltpu.make_async_copy(buf.at[k], dwo_hbm.at[e, rows, :], sem.at[k]))
+            copies[-1].start()
+        mine = pl.ds(pl.multiple_of(lax.axis_index("tp") * half, half), half)
+        for e in range(2):
+            part = mm(da_ref[e], wi_ref[e, mine, :], CONTRACT_LAST)
+            snear_ref[e] = part[0:blk]
+            sfar_ref[e] = part[blk:]
+        for copy in copies:
+            copy.wait()
+
+    return grad_out
 
 
 def y_tokens(picks_ref, ynear_ref, yfar0_ref, yfar1_ref, after_ref, y_ref):
@@ -285,32 +314,34 @@
     dwgt_ref[...] = (dwg[0] + dwg[1]) + (dwg[2] + dwg[3])
 
 
-def write_out(dwgt_ref, ymine_ref, ytheirs_ref, prob_ref, chosen_ref, out_hbm, dwgt_hbm, out_ref, sem):
+def write_out(dwgt_ref, ymine_ref, ytheirs_ref, prob_ref, chosen_ref, dlog_ref, wgt_ref, smine_ref,
+              out_hbm, dwgt_hbm, dx_hbm, rgrad_ref, out_ref, dx_ref, sem):
     half = ymine_ref.shape[1]
-    first = pltpu.make_async_copy(dwgt_ref, dwgt_hbm, sem.at[0])
-    first.start()
     tp = lax.axis_index("tp")
+    mine, theirs = [pl.ds(pl.multiple_of(side * half, half), half) for side in (tp, 1 - tp)]
+    copies = [pltpu.make_async_copy(src, dst, sem.at[k]) for k, (src, dst) in enumerate(
+        ((dwgt_ref, dwgt_hbm), (out_ref, out_hbm), (dx_ref, dx_hbm.at[:, mine])))]
+    copies[0].start()
     gate = jnp.sum(chosen_ref[...] * prob_ref[...], axis=1, keepdims=True)
-    for side, ref in ((tp, ymine_ref), (1 - tp, ytheirs_ref)):
-        out_ref[:, pl.ds(pl.multiple_of(side * half, half), half)] = (gate * ref[...].astype(F32)).astype(BF16)
-    second = pltpu.make_async_copy(out_ref, out_hbm, sem.at[1])
-    second.start()
-    first.wait()
-    second.wait()
-
-
-def write_dx(dlog_ref, wgt_ref, smine_ref, stheirs_ref, after_ref, dx_hbm, dx_ref, sem):
-    half = smine_ref.shape[1]
-    tp = lax.axis_index("tp")
-    for side, ref in ((tp, smine_ref), (1 - tp, stheirs_ref)):
-        cols = pl.ds(pl.multiple_of(side * half, half), half)
-        dx_ref[:, cols] = (ref[...].astype(F32) + mm(dlog_ref[...], wgt_ref[:, cols])).astype(BF16)
-    copy = pltpu.make_async_copy(dx_ref, dx_hbm, sem)
+    out_ref[:, mine] = (gate * ymine_ref[...].astype(F32)).astype(BF16)
+    out_ref[:, theirs] = (gate * ytheirs_ref[...].astype(F32)).astype(BF16)
+    copies[1].start()
+    dx_ref[...] = (smine_ref[...].astype(F32) + mm(dlog_ref[...], wgt_ref[:, mine])).astype(BF16)
+    copies[2].start()
+    rgrad_ref[...] = mm(dlog_ref[...], wgt_ref[:, theirs])
+    for copy in copies:
+        copy.wait()
+
+
+def write_dx(rgrad_ref, stheirs_ref, dx_in, dx_hbm, dx_ref, sem):
+    half = stheirs_ref.shape[1]
+    dx_ref[...] = (stheirs_ref[...].astype(F32) + rgrad_ref[...]).astype(BF16)
+    copy = pltpu.make_async_copy(dx_ref, dx_hbm.at[:, pl.ds(pl.multiple_of((1 - lax.axis_index("tp")) * half, half), half)], sem)
     copy.start()
     copy.wait()
 
 
-FIRST_PART = 12
+FIRST_PART = 14
 
 
 def solution(mesh):
@@ -332,25 +363,26 @@
         sds = jax.ShapeDtypeStruct
         dma = pltpu.SemaphoreType.DMA
 
-        h, da, xs, dys, sfar, snear, sfar_own, snear_own, ynear, yfar0, yfar1, picks, prob, chosen = pl.pallas_call(
+        h, da, xs, dys, sfar, snear, ynear, yfar0, yfar1, picks, prob, chosen, wi_v = pl.pallas_call(
             make_front(n_experts, capacity, cap),
             out_shape=(sds((le, rows, d_ff), BF16), sds((le, rows, d_ff), BF16), sds((le, rows, d_model), BF16),
-                       sds((le, rows, d_model), BF16), *[sds((le, blk, half), F32)] * 4,
+                       sds((le, rows, d_model), BF16), *[sds((le, blk, half), F32)] * 2,
                        sds((2 * blk, half), BF16), sds((blk, half), BF16), sds((blk, half), BF16),
-                       sds((4 * blk, n), BF16), sds((n, n_experts), F32), sds((n, n_experts), F32)),
+                       sds((4 * blk, n), BF16), sds((n, n_experts), F32), sds((n, n_experts), F32),
+                       sds((le, d_model, d_ff), BF16)),
             in_specs=[hbm] * 6,
-            out_specs=(vmem,) * 14,
+            out_specs=(vmem,) * 13,
             scratch_shapes=[
                 pltpu.VMEM((n, d_model), BF16), pltpu.VMEM((n, d_model), BF16), pltpu.VMEM((n_experts, d_model), BF16),
                 pltpu.VMEM((1, n), jnp.int32),
-                pltpu.VMEM((le, d_model, d_ff), BF16), pltpu.VMEM((le, d_ff, d_model), BF16),
+                pltpu.VMEM((le, d_ff, d_model), BF16),
                 pltpu.VMEM((3, le, cap, d_model), BF16), pltpu.VMEM((3, le, cap, d_model), BF16),
                 pltpu.VMEM((le, rows, d_ff), F32),
-                pltpu.VMEM((2, le, blk, half), F32), pltpu.VMEM((le, rows, half), F32), pltpu.VMEM((2, le, blk, half), F32),
+                *[pltpu.VMEM((le, rows, half), F32)] * 3,
                 pltpu.VMEM((blk, half), BF16), pltpu.VMEM((blk, half), BF16),
-                dma((4,)), dma((2, le)), dma((3, le)), dma((3, le)), dma((3, le)), dma((3, le)), dma((2, le)), dma((2, le)), dma, dma,
+                dma((4,)), dma((3, le)), dma, dma((2, le)), dma, dma((2, le)), dma((le, 3)), dma((le, 3)), dma, dma,
             ],
-            compiler_params=pltpu.CompilerParams(collective_id=0, has_side_effects=True, vmem_limit_bytes=40 * 2**20),
+            compiler_params=pltpu.CompilerParams(collective_id=0, has_side_effects=True, vmem_limit_bytes=32 * 2**20),
             name="front",
         )(*[pltpu.with_memory_space_constraint(v, pltpu.HBM) for v in (tokens, grad_out, wgt, idx_row, w_in, w_out)])
 
@@ -380,8 +412,13 @@
         out_size, in_size = d_ff // 8, d_model // 8
         out_pieces = [(e, c * out_size) for e in range(le) for c in range(8)]
         in_pieces = [(e, c * in_size) for e in range(le) for c in range(8)]
-        dwo, done = weight_grad(h, dys, ynear, out_pieces, out_size, True)
-        ymine = local(y_tokens, sds((n, half), BF16), [vmem] * 5, vmem, (picks, ynear, yland0, yland1, done))
+        dwo, sfar_own, snear_own = local(
+            make_grad_out(out_pieces), (sds((le, d_ff, d_model), F32), *[sds((le, blk, half), F32)] * 2), [vmem] * 4,
+            (hbm, vmem, vmem), (h, dys, da, wi_v),
+            [pltpu.VMEM((len(out_pieces), out_size, d_model), F32), dma((len(out_pieces),))], 24,
+            cost_estimate=pl.CostEstimate(flops=2 * rows * le * d_ff * d_model, bytes_accessed=4 * le * d_ff * d_model,
+                                          transcendentals=0))
+        ymine = local(y_tokens, sds((n, half), BF16), [vmem] * 5, vmem, (picks, ynear, yland0, yland1, sfar_own))
         ytheirs = lax.ppermute(ymine, "tp", swap)
         sblocks = local(make_blocks(cap), sds((2 * blk, half), BF16), [vmem] * 3, vmem, (sfar_own, sfar_recv, ymine))
         sfar_land = lax.ppermute(sblocks, "ep", across)
@@ -402,10 +439,13 @@
             compiler_params=pltpu.CompilerParams(collective_id=2, has_side_effects=True, vmem_limit_bytes=8 * 2**20),
             name="router_grad",
         )(tokens, grad_out, prob, chosen, ymine, ytheirs, done)
-        out, dwgt = local(write_out, (sds((n, d_model), BF16), sds((n_experts, d_model), F32)), [vmem] * 5, (hbm,) * 2,
-                          (dwgt_v, ymine, ytheirs, prob, chosen), [pltpu.VMEM((n, d_model), BF16), dma((2,))])
-        dx = local(write_dx, sds((n, d_model), BF16), [vmem] * 5, hbm, (dlog, wgt, smine, stheirs, dwgt_v),
-                   [pltpu.VMEM((n, d_model), BF16), dma])
+        tok = sds((n, d_model), BF16)
+        out, dwgt, dx, rgrad = local(
+            write_out, (tok, sds((n_experts, d_model), F32), tok, sds((n, half), F32)), [vmem] * 8, (hbm, hbm, hbm, vmem),
+            (dwgt_v, ymine, ytheirs, prob, chosen, dlog, wgt, smine),
+            [pltpu.VMEM((n, d_model), BF16), pltpu.VMEM((n, half), BF16), dma((3,))])
+        dx = local(write_dx, tok, [vmem, vmem, hbm], hbm, (rgrad, stheirs, dx),
+                   [pltpu.VMEM((n, half), BF16), dma], input_output_aliases={2: 0})
         return out, dx, dwi, dwo, dwgt.T
 
     in_specs = (row_spec, row_spec, P(None, None), P("ep", None, "tp"), P("ep", "tp", None), P(("dp", "ep")))

time: 53.4 us -> 53.2 us (level)
  transfers between devices with their start and end apart: 7 -> 7, of which waited for: 1 -> 2; matrix products, arithmetic and copies ran while one was open for 0% -> 0% of each run, Pallas kernels for 39% -> 40%
where the time goes in v1:
time: 53.2 us; the launch traced here: 53.1 us
  Pallas kernels  44.8 us (84%)
  starting transfers between devices  6.64 us (12%)
  between operations  0.93 us (2%)
  waiting for transfers between devices  0.73 us (1%)
    pallas_call x1, Pallas kernels, local_block(): pl.pallas_call(make_front(n_experts, capacity, cap), out_shape=(sds((le,...  23 us
    pallas_call x7, Pallas kernels, local(): pl.pallas_call(kernel, out_shape=out_shape, in_specs=ins, out_specs=outs,...  15.9 us
    pallas_call x1, Pallas kernels, local_block(): pl.pallas_call(router_grad, out_shape=(sds((n, n_experts), BF16), sds((n_...  4.14 us
    pallas_call x1, Pallas kernels, local_block(): pl.pallas_call(make_near_return(cap), out_shape=sds((n, half), BF16), in_...  1.77 us
    ppermute x1, starting transfers between devices, local_block(): snear_recv = lax.ppermute(snear, 'tp', swap)  1.48 us
    ppermute x1, starting transfers between devices, local_block(): sfar_land = lax.ppermute(sblocks, 'ep', across)  1.27 us
    ppermute x1, starting transfers between devices, local_block(): stheirs = lax.ppermute(smine, 'tp', swap)  1.27 us
    ppermute x1, starting transfers between devices, local_block(): yland0 = lax.ppermute(yfar0, 'ep', across)  1.25 us
  transfers between devices with their start and end apart: 7, of which 2 were waited for; matrix products, arithmetic and copies ran while one was open for 0% of the time, Pallas kernels for 40%

profile of v1, /device:TPU:0, one launch (start us, length us, event | category | flops | bytes accessed | tf_op | source)
XLA Modules:
  0.0 53.1 jit_solution(9941544596724901123)
XLA Ops:
  0.6 23.0 %front.1 = (bf16[2,160,2048]{2,1,0:T(8,128)(2,1)S(1)}, bf16[2,160,2048]{2,1,0:T(8,128)(2,1)S(1)}, bf16[2,160,1024]{2,1,0:T(8,128)(2,1)S(1)}, bf16[2,160,1024]{2,...) custom-call(bf16[256,1024]{1,0:T(8,128)(2,1)} %x_ref.1, ...), custom_call_target="tpu_custom_call" | custom-call | tf_op jit(solution)/shard_map/front/pallas_call | solution.py:366
  23.6 0.6 %collective-permute-start.3 = (f32[2,80,512]{2,1,0:T(8,128)S(1)}, f32[2,80,512]{2,1,0:T(8,128)S(1)}, u32[]{:S(2)}, u32[]{:S(2)}) collective-permute-start(f32[2,80,512]{2,1,0:T(8,128)S(1)} %get-tuple-element.43), channel_id=1, source_target_pairs={{0,4},{4,0},{1,5},{5,1},{2,6},{6,2},{3,7},{7,3}} | collective-permute-start | bytes 983048 | tf_op jit(solution)/shard_map/ppermute | solution.py:391
  24.2 1.5 %collective-permute-start.5 = (f32[2,80,512]{2,1,0:T(8,128)S(1)}, f32[2,80,512]{2,1,0:T(8,128)S(1)}, u32[]{:S(2)}, u32[]{:S(2)}) collective-permute-start(f32[2,80,512]{2,1,0:T(8,128)S(1)} %get-tuple-element.45), channel_id=1, source_target_pairs={{0,4},{4,0},{1,5},{5,1},{2,6},{6,2},{3,7},{7,3}} | collective-permute-start | bytes 983048 | tf_op jit(solution)/shard_map/ppermute | solution.py:392
  25.7 1.3 %collective-permute-start = (bf16[80,512]{1,0:T(8,128)(2,1)S(1)}, bf16[80,512]{1,0:T(8,128)(2,1)S(1)}, u32[]{:S(2)}, u32[]{:S(2)}) collective-permute-start(bf16[80,512]{1,0:T(8,128)(2,1)S(1)} %get-tuple-element.35), channel_id=1, source_target_pairs={{0,2},{2,0},{1,3},{3,1},{4,6},{6,4},{5,7},{7,5}} | collective-permute-start | bytes 245768 | tf_op jit(solution)/shard_map/ppermute | solution.py:393
  26.9 0.0 collective-permute-start.1
  27.0 6.3 %shard_map.101 = (f32[2,2048,1024]{2,1,0:T(8,128)}, f32[2,80,512]{2,1,0:T(8,128)S(1)}, f32[2,80,512]{2,1,0:T(8,128)S(1)}) custom-call(bf16[2,160,2048]{2,1,0:T(8,128)(2,1)S(1)} %get-tuple-element.37.h_ref, bf16[2,160,1024]{2,1,0:T(8,128)(2,1)S(1)} %get-tuple-element.38.dys_ref, bf16[2,160,2048]{2,1,0:T(8,128)(2,1)S(1)} %get-tuple-element.39.da_ref.right_ref, ...), custom_call_target="tpu_custom_call" | custom-call | flops 1342177280 | bytes 16777216 | tf_op jit(solution)/shard_map/pallas_call | solution.py:397
  33.2 0.0 collective-permute-done.yfar0_ref
  33.3 0.0 collective-permute-done.1.yfar1_ref
  33.3 0.3 shard_map.102.after_ref.ymine_ref
  33.6 0.7 %collective-permute-done.3.recv_ref = f32[2,80,512]{2,1,0:T(8,128)S(1)} collective-permute-done((f32[2,80,512]{2,1,0:T(8,128)S(1)}, f32[2,80,512]{2,1,0:T(8,128)S(1)}, u32[]{:S(2)}, u32[]{:S(2)}) %collective-permute-start.3) | collective-permute-done | bytes 327712 | tf_op jit(solution)/shard_map/ppermute | solution.py:391
  34.3 1.3 %collective-permute-start.4 = (bf16[160,512]{1,0:T(8,128)(2,1)S(1)}, bf16[160,512]{1,0:T(8,128)(2,1)S(1)}, u32[]{:S(2)}, u32[]{:S(2)}) collective-permute-start(bf16[160,512]{1,0:T(8,128)(2,1)S(1)} %shard_map.103.after_ref), channel_id=1, source_target_pairs={{0,2},{2,0},{1,3},{3,1},{4,6},{6,4},{5,7},{7,5}} | collective-permute-start | bytes 491528 | tf_op jit(solution)/shard_map/ppermute | solution.py:424
  35.6 0.8 %collective-permute-start.2 = (bf16[256,512]{1,0:T(8,128)(2,1)S(1)}, bf16[256,512]{1,0:T(8,128)(2,1)S(1)}, u32[]{:S(2)}, u32[]{:S(2)}) collective-permute-start(bf16[256,512]{1,0:T(8,128)(2,1)S(1)} %shard_map.102.after_ref.ymine_ref), channel_id=1, source_target_pairs={{0,4},{4,0},{1,5},{5,1},{2,6},{6,2},{3,7},{7,3}} | collective-permute-start | bytes 786440 | tf_op jit(solution)/shard_map/ppermute | solution.py:422
  36.3 5.6 %shard_map.104 = (f32[2,1024,2048]{2,1,0:T(8,128)}, f32[8,128]{1,0:T(8,128)S(1)}) custom-call(bf16[2,160,1024]{2,1,0:T(8,128)(2,1)S(1)} %get-tuple-element.42.left_ref, bf16[2,160,2048]{2,1,0:T(8,128)(2,1)S(1)} %get-tuple-element.39.da_ref.right_ref, bf16[160,512]{1,0:T(8,128)(2,1)S(1)} %shard_map.103.after_ref), custom_call_target="tpu_custom_call" | custom-call | flops 1174405120 | bytes 14680064 | tf_op jit(solution)/shard_map/pallas_call | solution.py:397
  42.0 0.0 collective-permute-done.5.srecv_ref
  42.0 0.0 collective-permute-done.4.sfar_ref
  42.0 1.8 %near_return.1.after_ref.smine_ref = bf16[256,512]{1,0:T(8,128)(2,1)S(1)} custom-call(bf16[320,256]{1,0:T(8,128)(2,1)S(1)} %get-tuple-element.33.picks_ref, bf16[160,512]{1,0:T(8,128)(2,1)S(1)} %collective-permute-done.4.sfar_ref, f32[2,80,512]{2,1,0:T(8,128)S(1)} %get-tuple-element.44.sown_ref, f32[2,80,512]{2,1,0:T(8,128)S(1)} %collective-permute-done.5.srecv_ref, ...), custom_call_target="tpu_custom_call" | custom-call | tf_op jit(solution)/shard_map/near_return/pallas_call | solution.py:427
  43.8 1.3 %collective-permute-start.6 = (bf16[256,512]{1,0:T(8,128)(2,1)S(1)}, bf16[256,512]{1,0:T(8,128)(2,1)S(1)}, u32[]{:S(2)}, u32[]{:S(2)}) collective-permute-start(bf16[256,512]{1,0:T(8,128)(2,1)S(1)} %near_return.1.after_ref.smine_ref), channel_id=1, source_target_pairs={{0,4},{4,0},{1,5},{5,1},{2,6},{6,2},{3,7},{7,3}} | collective-permute-start | bytes 786440 | tf_op jit(solution)/shard_map/ppermute | solution.py:433
  45.1 0.0 copy-start
  45.1 0.0 copy-start.1
  45.1 0.0 copy-start.2
  45.1 1.7 %shard_map.105 = (f32[2,1024,2048]{2,1,0:T(8,128)}, f32[8,128]{1,0:T(8,128)S(1)}) custom-call(bf16[2,160,1024]{2,1,0:T(8,128)(2,1)S(1)} %get-tuple-element.42.left_ref, bf16[2,160,2048]{2,1,0:T(8,128)(2,1)S(1)} %get-tuple-element.39.da_ref.right_ref, bf16[256,512]{1,0:T(8,128)(2,1)S(1)} %near_return.1.after_ref.smine_ref, ...), custom_call_target="tpu_custom_call", output_to_operand_aliasing={{0}: (3, {})} | custom-call | flops 167772160 | bytes 2097152 | tf_op jit(solution)/shard_map/pallas_call | solution.py:397
  46.7 0.0 collective-permute-done.2.ytheirs_ref
  46.7 0.0 copy-done
  46.8 0.0 copy-done.1
  46.8 4.1 %router_grad.1 = (bf16[256,8]{1,0:T(8,128)(2,1)S(1)}, f32[8,1024]{1,0:T(8,128)S(1)}) custom-call(bf16[256,1024]{1,0:T(8,128)(2,1)S(1)} %copy-done, bf16[256,1024]{1,0:T(8,128)(2,1)S(1)} %copy-done.1, f32[256,8]{1,0:T(8,128)S(1)} %get-tuple-element.31.prob_ref, f32[256,8]{1,0:T(8,128)S(1)} %get-tuple-element.32.chosen_ref, ...), custom_call_target="tpu_custom_call" | custom-call | tf_op jit(solution)/shard_map/router_grad/pallas_call | solution.py:435
  50.9 0.0 copy-done.2
  50.9 1.2 %shard_map.106 = (bf16[256,1024]{1,0:T(8,128)(2,1)}, f32[8,1024]{1,0:T(8,128)}, bf16[256,1024]{1,0:T(8,128)(2,1)}, f32[256,512]{1,0:T(8,128)S(1)}) custom-call(f32[8,1024]{1,0:T(8,128)S(1)} %get-tuple-element.49.dwgt_ref, bf16[256,512]{1,0:T(8,128)(2,1)S(1)} %shard_map.102.after_ref.ymine_ref, bf16[256,512]{1,0:T(8,128)(2,1)S(1)} %collective-permute-done.2.ytheirs_ref, ...), custom_call_target="tpu_custom_call" | custom-call | tf_op jit(solution)/shard_map/pallas_call | solution.py:397
  52.1 0.1 collective-permute-done.6.stheirs_ref
  52.2 0.8 %shard_map.107 = bf16[256,1024]{1,0:T(8,128)(2,1)} custom-call(f32[256,512]{1,0:T(8,128)S(1)} %get-tuple-element.52.rgrad_ref, bf16[256,512]{1,0:T(8,128)(2,1)S(1)} %collective-permute-done.6.stheirs_ref, bf16[256,1024]{1,0:T(8,128)(2,1)} %get-tuple-element.53.dx_in), custom_call_target="tpu_custom_call", output_to_operand_aliasing={{}: (2, {})} | custom-call | tf_op jit(solution)/shard_map/pallas_call | solution.py:397
  (1 shorter events, 0.0 us)
Async XLA Ops:
  23.6 10.6 %collective-permute-start.3 = (f32[2,80,512]{2,1,0:T(8,128)S(1)}, f32[2,80,512]{2,1,0:T(8,128)S(1)}, u32[]{:S(2)}, u32[]{:S(2)}) collective-permute-start(f32[2,80,512]{2,1,0:T(8,128)S(1)} %get-tuple-element.43), channel_id=1, source_target_pairs={{0,4},{4,0},{1,5},{5,1},{2,6},{6,2},{3,7},{7,3}} | collective-permute-start | bytes 983048 | tf_op jit(solution)/shard_map/ppermute | solution.py:391
  24.2 17.8 %collective-permute-start.5 = (f32[2,80,512]{2,1,0:T(8,128)S(1)}, f32[2,80,512]{2,1,0:T(8,128)S(1)}, u32[]{:S(2)}, u32[]{:S(2)}) collective-permute-start(f32[2,80,512]{2,1,0:T(8,128)S(1)} %get-tuple-element.45), channel_id=1, source_target_pairs={{0,4},{4,0},{1,5},{5,1},{2,6},{6,2},{3,7},{7,3}} | collective-permute-start | bytes 983048 | tf_op jit(solution)/shard_map/ppermute | solution.py:392
  25.7 7.6 %collective-permute-start = (bf16[80,512]{1,0:T(8,128)(2,1)S(1)}, bf16[80,512]{1,0:T(8,128)(2,1)S(1)}, u32[]{:S(2)}, u32[]{:S(2)}) collective-permute-start(bf16[80,512]{1,0:T(8,128)(2,1)S(1)} %get-tuple-element.35), channel_id=1, source_target_pairs={{0,2},{2,0},{1,3},{3,1},{4,6},{6,4},{5,7},{7,5}} | collective-permute-start | bytes 245768 | tf_op jit(solution)/shard_map/ppermute | solution.py:393
  26.9 6.3 %collective-permute-start.1 = (bf16[80,512]{1,0:T(8,128)(2,1)S(1)}, bf16[80,512]{1,0:T(8,128)(2,1)S(1)}, u32[]{:S(2)}, u32[]{:S(2)}) collective-permute-start(bf16[80,512]{1,0:T(8,128)(2,1)S(1)} %get-tuple-element.36), channel_id=1, source_target_pairs={{0,3},{3,0},{1,2},{2,1},{4,7},{7,4},{5,6},{6,5}} | collective-permute-start | bytes 245768 | tf_op jit(solution)/shard_map/ppermute | solution.py:394
  34.3 7.7 %collective-permute-start.4 = (bf16[160,512]{1,0:T(8,128)(2,1)S(1)}, bf16[160,512]{1,0:T(8,128)(2,1)S(1)}, u32[]{:S(2)}, u32[]{:S(2)}) collective-permute-start(bf16[160,512]{1,0:T(8,128)(2,1)S(1)} %shard_map.103.after_ref), channel_id=1, source_target_pairs={{0,2},{2,0},{1,3},{3,1},{4,6},{6,4},{5,7},{7,5}} | collective-permute-start | bytes 491528 | tf_op jit(solution)/shard_map/ppermute | solution.py:424
  35.6 11.2 %collective-permute-start.2 = (bf16[256,512]{1,0:T(8,128)(2,1)S(1)}, bf16[256,512]{1,0:T(8,128)(2,1)S(1)}, u32[]{:S(2)}, u32[]{:S(2)}) collective-permute-start(bf16[256,512]{1,0:T(8,128)(2,1)S(1)} %shard_map.102.after_ref.ymine_ref), channel_id=1, source_target_pairs={{0,4},{4,0},{1,5},{5,1},{2,6},{6,2},{3,7},{7,3}} | collective-permute-start | bytes 786440 | tf_op jit(solution)/shard_map/ppermute | solution.py:422
  43.8 8.4 %collective-permute-start.6 = (bf16[256,512]{1,0:T(8,128)(2,1)S(1)}, bf16[256,512]{1,0:T(8,128)(2,1)S(1)}, u32[]{:S(2)}, u32[]{:S(2)}) collective-permute-start(bf16[256,512]{1,0:T(8,128)(2,1)S(1)} %near_return.1.after_ref.smine_ref), channel_id=1, source_target_pairs={{0,4},{4,0},{1,5},{5,1},{2,6},{6,2},{3,7},{7,3}} | collective-permute-start | bytes 786440 | tf_op jit(solution)/shard_map/ppermute | solution.py:433
  45.1 1.7 %copy-start = (bf16[256,1024]{1,0:T(8,128)(2,1)S(1)}, bf16[256,1024]{1,0:T(8,128)(2,1)}, u32[]{:S(2)}) copy-start(bf16[256,1024]{1,0:T(8,128)(2,1)} %x_ref.1) | copy-start | bytes 1572868
  45.1 1.7 %copy-start.1 = (bf16[256,1024]{1,0:T(8,128)(2,1)S(1)}, bf16[256,1024]{1,0:T(8,128)(2,1)}, u32[]{:S(2)}) copy-start(bf16[256,1024]{1,0:T(8,128)(2,1)} %gy_ref.1) | copy-start | bytes 1572868
  45.1 5.8 %copy-start.2 = (bf16[1024,8]{0,1:T(8,128)(2,1)S(1)}, bf16[1024,8]{0,1:T(8,128)(2,1)}, u32[]{:S(2)}) copy-start(bf16[1024,8]{0,1:T(8,128)(2,1)} %param.8) | copy-start | bytes 49156

commit v2 on v1

--- a/solution.py
+++ b/solution.py
@@ -100,7 +100,7 @@
                 loads[name, e] = pltpu.make_async_copy(wo_hbm.at[e, :, cols], wo.at[e, :, cols], wsem.at[1 + k, e])
         loads["i", 0].start()
 
-        xc, dc, yc = {}, {}, {}
+        xc, dc = {}, {}
 
         def dispatch(v, g, e, buf, rows_ref, ssem, rsem, made):
             first = [peers[2 * g + q] * blk + e * cap for q in range(2)]
@@ -139,7 +139,7 @@
             if first == 0:
                 loads["theirs", e].wait()
             ypeer[e, rows, :] = mm(h_ref[e, rows, :], wo[e, :, theirs])
-            yc[e, first] = send(ypeer.at[e, rows, :], yrecv.at[e, rows, :], y_s.at[e, first], y_r.at[e, first], {"tp": tp_peer})
+            send(ypeer.at[e, rows, :], yrecv.at[e, rows, :], y_s, y_r.at[e, first // 2], {"tp": tp_peer})
 
         small[0].wait()
         hot, slot = route(idx_ref[...], capacity, n_experts, cap)
@@ -171,9 +171,8 @@
         def y_blocks(g):
             rows = far if g else near
             for e in range(2):
-                for r in (2 * g, 2 * g + 1):
-                    if (e, r) in yc:
-                        yc[e, r].wait()
+                part = yrecv.at[e, rows, :]
+                pltpu.make_async_copy(part, part, y_r.at[e, g]).wait()
             both = [yown[e, rows, :] + yrecv[e, rows, :] for e in range(2)]
             return [jnp.concatenate([both[e][q * cap:(q + 1) * cap] for e in range(2)], axis=0).astype(BF16) for q in range(2)]
 
@@ -212,7 +211,7 @@
         bc.wait()
         ynear_ref[far, :] = yland[...]
         yfar0_ref[...], yfar1_ref[...] = y_blocks(1)
-        for sent, sem in ((xsend, x_s), (dysend, d_s)):
+        for sent, sem in ((xsend, x_s), (dysend, d_s), (ypeer, y_s)):
             pltpu.make_async_copy(sent, sent, sem).wait()
 
     return front
@@ -380,7 +379,7 @@
                 pltpu.VMEM((le, rows, d_ff), F32),
                 *[pltpu.VMEM((le, rows, half), F32)] * 3,
                 pltpu.VMEM((blk, half), BF16), pltpu.VMEM((blk, half), BF16),
-                dma((4,)), dma((3, le)), dma, dma((2, le)), dma, dma((2, le)), dma((le, 3)), dma((le, 3)), dma, dma,
+                dma((4,)), dma((3, le)), dma, dma((2, le)), dma, dma((2, le)), dma, dma((le, 2)), dma, dma,
             ],
             compiler_params=pltpu.CompilerParams(collective_id=0, has_side_effects=True, vmem_limit_bytes=32 * 2**20),
             name="front",

time: 53.2 us -> 53.1 us (level)
  no operation moved by 1% of the time
where the time goes in v2:
time: 53.1 us; the launch traced here: 53 us
  Pallas kernels  44.7 us (84%)
  starting transfers between devices  6.62 us (12%)
  between operations  0.93 us (2%)
  waiting for transfers between devices  0.74 us (1%)
    pallas_call x1, Pallas kernels, local_block(): pl.pallas_call(make_front(n_experts, capacity, cap), out_shape=(sds((le,...  22.9 us
    pallas_call x7, Pallas kernels, local(): pl.pallas_call(kernel, out_shape=out_shape, in_specs=ins, out_specs=outs,...  15.9 us
    pallas_call x1, Pallas kernels, local_block(): pl.pallas_call(router_grad, out_shape=(sds((n, n_experts), BF16), sds((n_...  4.14 us
    pallas_call x1, Pallas kernels, local_block(): pl.pallas_call(make_near_return(cap), out_shape=sds((n, half), BF16), in_...  1.77 us
    ppermute x1, starting transfers between devices, local_block(): snear_recv = lax.ppermute(snear, 'tp', swap)  1.48 us
    ppermute x1, starting transfers between devices, local_block(): sfar_land = lax.ppermute(sblocks, 'ep', across)  1.27 us
    ppermute x1, starting transfers between devices, local_block(): stheirs = lax.ppermute(smine, 'tp', swap)  1.26 us
    ppermute x1, starting transfers between devices, local_block(): yland0 = lax.ppermute(yfar0, 'ep', across)  1.25 us
  transfers between devices with their start and end apart: 7, of which 2 were waited for; matrix products, arithmetic and copies ran while one was open for 0% of the time, Pallas kernels for 40%

profile of v2, /device:TPU:0, one launch (start us, length us, event | category | flops | bytes accessed | tf_op | source)
XLA Modules:
  0.0 53.0 jit_solution(16428895858741014895)
XLA Ops:
  0.6 22.9 %front.1 = (bf16[2,160,2048]{2,1,0:T(8,128)(2,1)S(1)}, bf16[2,160,2048]{2,1,0:T(8,128)(2,1)S(1)}, bf16[2,160,1024]{2,1,0:T(8,128)(2,1)S(1)}, bf16[2,160,1024]{2,...) custom-call(bf16[256,1024]{1,0:T(8,128)(2,1)} %x_ref.1, ...), custom_call_target="tpu_custom_call" | custom-call | tf_op jit(solution)/shard_map/front/pallas_call | solution.py:365
  23.6 0.6 %collective-permute-start.3 = (f32[2,80,512]{2,1,0:T(8,128)S(1)}, f32[2,80,512]{2,1,0:T(8,128)S(1)}, u32[]{:S(2)}, u32[]{:S(2)}) collective-permute-start(f32[2,80,512]{2,1,0:T(8,128)S(1)} %get-tuple-element.43), channel_id=1, source_target_pairs={{0,4},{4,0},{1,5},{5,1},{2,6},{6,2},{3,7},{7,3}} | collective-permute-start | bytes 983048 | tf_op jit(solution)/shard_map/ppermute | solution.py:390
  24.2 1.5 %collective-permute-start.5 = (f32[2,80,512]{2,1,0:T(8,128)S(1)}, f32[2,80,512]{2,1,0:T(8,128)S(1)}, u32[]{:S(2)}, u32[]{:S(2)}) collective-permute-start(f32[2,80,512]{2,1,0:T(8,128)S(1)} %get-tuple-element.45), channel_id=1, source_target_pairs={{0,4},{4,0},{1,5},{5,1},{2,6},{6,2},{3,7},{7,3}} | collective-permute-start | bytes 983048 | tf_op jit(solution)/shard_map/ppermute | solution.py:391
  25.6 1.3 %collective-permute-start = (bf16[80,512]{1,0:T(8,128)(2,1)S(1)}, bf16[80,512]{1,0:T(8,128)(2,1)S(1)}, u32[]{:S(2)}, u32[]{:S(2)}) collective-permute-start(bf16[80,512]{1,0:T(8,128)(2,1)S(1)} %get-tuple-element.35), channel_id=1, source_target_pairs={{0,2},{2,0},{1,3},{3,1},{4,6},{6,4},{5,7},{7,5}} | collective-permute-start | bytes 245768 | tf_op jit(solution)/shard_map/ppermute | solution.py:392
  26.9 0.0 collective-permute-start.1
  26.9 6.3 %shard_map.101 = (f32[2,2048,1024]{2,1,0:T(8,128)}, f32[2,80,512]{2,1,0:T(8,128)S(1)}, f32[2,80,512]{2,1,0:T(8,128)S(1)}) custom-call(bf16[2,160,2048]{2,1,0:T(8,128)(2,1)S(1)} %get-tuple-element.37.h_ref, bf16[2,160,1024]{2,1,0:T(8,128)(2,1)S(1)} %get-tuple-element.38.dys_ref, bf16[2,160,2048]{2,1,0:T(8,128)(2,1)S(1)} %get-tuple-element.39.da_ref.right_ref, ...), custom_call_target="tpu_custom_call" | custom-call | flops 1342177280 | bytes 16777216 | tf_op jit(solution)/shard_map/pallas_call | solution.py:396
  33.2 0.0 collective-permute-done.yfar0_ref
  33.2 0.0 collective-permute-done.1.yfar1_ref
  33.2 0.3 shard_map.102.after_ref.ymine_ref
  33.5 0.7 %collective-permute-done.3.recv_ref = f32[2,80,512]{2,1,0:T(8,128)S(1)} collective-permute-done((f32[2,80,512]{2,1,0:T(8,128)S(1)}, f32[2,80,512]{2,1,0:T(8,128)S(1)}, u32[]{:S(2)}, u32[]{:S(2)}) %collective-permute-start.3) | collective-permute-done | bytes 327712 | tf_op jit(solution)/shard_map/ppermute | solution.py:390
  34.2 1.3 %collective-permute-start.4 = (bf16[160,512]{1,0:T(8,128)(2,1)S(1)}, bf16[160,512]{1,0:T(8,128)(2,1)S(1)}, u32[]{:S(2)}, u32[]{:S(2)}) collective-permute-start(bf16[160,512]{1,0:T(8,128)(2,1)S(1)} %shard_map.103.after_ref), channel_id=1, source_target_pairs={{0,2},{2,0},{1,3},{3,1},{4,6},{6,4},{5,7},{7,5}} | collective-permute-start | bytes 491528 | tf_op jit(solution)/shard_map/ppermute | solution.py:423
  35.5 0.8 %collective-permute-start.2 = (bf16[256,512]{1,0:T(8,128)(2,1)S(1)}, bf16[256,512]{1,0:T(8,128)(2,1)S(1)}, u32[]{:S(2)}, u32[]{:S(2)}) collective-permute-start(bf16[256,512]{1,0:T(8,128)(2,1)S(1)} %shard_map.102.after_ref.ymine_ref), channel_id=1, source_target_pairs={{0,4},{4,0},{1,5},{5,1},{2,6},{6,2},{3,7},{7,3}} | collective-permute-start | bytes 786440 | tf_op jit(solution)/shard_map/ppermute | solution.py:421
  36.3 5.6 %shard_map.104 = (f32[2,1024,2048]{2,1,0:T(8,128)}, f32[8,128]{1,0:T(8,128)S(1)}) custom-call(bf16[2,160,1024]{2,1,0:T(8,128)(2,1)S(1)} %get-tuple-element.42.left_ref, bf16[2,160,2048]{2,1,0:T(8,128)(2,1)S(1)} %get-tuple-element.39.da_ref.right_ref, bf16[160,512]{1,0:T(8,128)(2,1)S(1)} %shard_map.103.after_ref), custom_call_target="tpu_custom_call" | custom-call | flops 1174405120 | bytes 14680064 | tf_op jit(solution)/shard_map/pallas_call | solution.py:396
  41.9 0.0 collective-permute-done.5.srecv_ref
  41.9 0.0 collective-permute-done.4.sfar_ref
  42.0 1.8 %near_return.1.after_ref.smine_ref = bf16[256,512]{1,0:T(8,128)(2,1)S(1)} custom-call(bf16[320,256]{1,0:T(8,128)(2,1)S(1)} %get-tuple-element.33.picks_ref, bf16[160,512]{1,0:T(8,128)(2,1)S(1)} %collective-permute-done.4.sfar_ref, f32[2,80,512]{2,1,0:T(8,128)S(1)} %get-tuple-element.44.sown_ref, f32[2,80,512]{2,1,0:T(8,128)S(1)} %collective-permute-done.5.srecv_ref, ...), custom_call_target="tpu_custom_call" | custom-call | tf_op jit(solution)/shard_map/near_return/pallas_call | solution.py:426
  43.7 1.3 %collective-permute-start.6 = (bf16[256,512]{1,0:T(8,128)(2,1)S(1)}, bf16[256,512]{1,0:T(8,128)(2,1)S(1)}, u32[]{:S(2)}, u32[]{:S(2)}) collective-permute-start(bf16[256,512]{1,0:T(8,128)(2,1)S(1)} %near_return.1.after_ref.smine_ref), channel_id=1, source_target_pairs={{0,4},{4,0},{1,5},{5,1},{2,6},{6,2},{3,7},{7,3}} | collective-permute-start | bytes 786440 | tf_op jit(solution)/shard_map/ppermute | solution.py:432
  45.0 0.0 copy-start
  45.0 0.0 copy-start.1
  45.0 0.0 copy-start.2
  45.0 1.7 %shard_map.105 = (f32[2,1024,2048]{2,1,0:T(8,128)}, f32[8,128]{1,0:T(8,128)S(1)}) custom-call(bf16[2,160,1024]{2,1,0:T(8,128)(2,1)S(1)} %get-tuple-element.42.left_ref, bf16[2,160,2048]{2,1,0:T(8,128)(2,1)S(1)} %get-tuple-element.39.da_ref.right_ref, bf16[256,512]{1,0:T(8,128)(2,1)S(1)} %near_return.1.after_ref.smine_ref, ...), custom_call_target="tpu_custom_call", output_to_operand_aliasing={{0}: (3, {})} | custom-call | flops 167772160 | bytes 2097152 | tf_op jit(solution)/shard_map/pallas_call | solution.py:396
  46.7 0.0 collective-permute-done.2.ytheirs_ref
  46.7 0.0 copy-done
  46.7 0.0 copy-done.1
  46.7 4.1 %router_grad.1 = (bf16[256,8]{1,0:T(8,128)(2,1)S(1)}, f32[8,1024]{1,0:T(8,128)S(1)}) custom-call(bf16[256,1024]{1,0:T(8,128)(2,1)S(1)} %copy-done, bf16[256,1024]{1,0:T(8,128)(2,1)S(1)} %copy-done.1, f32[256,8]{1,0:T(8,128)S(1)} %get-tuple-element.31.prob_ref, f32[256,8]{1,0:T(8,128)S(1)} %get-tuple-element.32.chosen_ref, ...), custom_call_target="tpu_custom_call" | custom-call | tf_op jit(solution)/shard_map/router_grad/pallas_call | solution.py:434
  50.8 0.0 copy-done.2
  50.8 1.2 %shard_map.106 = (bf16[256,1024]{1,0:T(8,128)(2,1)}, f32[8,1024]{1,0:T(8,128)}, bf16[256,1024]{1,0:T(8,128)(2,1)}, f32[256,512]{1,0:T(8,128)S(1)}) custom-call(f32[8,1024]{1,0:T(8,128)S(1)} %get-tuple-element.49.dwgt_ref, bf16[256,512]{1,0:T(8,128)(2,1)S(1)} %shard_map.102.after_ref.ymine_ref, bf16[256,512]{1,0:T(8,128)(2,1)S(1)} %collective-permute-done.2.ytheirs_ref, ...), custom_call_target="tpu_custom_call" | custom-call | tf_op jit(solution)/shard_map/pallas_call | solution.py:396
  52.0 0.1 collective-permute-done.6.stheirs_ref
  52.1 0.8 %shard_map.107 = bf16[256,1024]{1,0:T(8,128)(2,1)} custom-call(f32[256,512]{1,0:T(8,128)S(1)} %get-tuple-element.52.rgrad_ref, bf16[256,512]{1,0:T(8,128)(2,1)S(1)} %collective-permute-done.6.stheirs_ref, bf16[256,1024]{1,0:T(8,128)(2,1)} %get-tuple-element.53.dx_in), custom_call_target="tpu_custom_call", output_to_operand_aliasing={{}: (2, {})} | custom-call | tf_op jit(solution)/shard_map/pallas_call | solution.py:396
  (1 shorter events, 0.0 us)
Async XLA Ops:
  23.6 10.6 %collective-permute-start.3 = (f32[2,80,512]{2,1,0:T(8,128)S(1)}, f32[2,80,512]{2,1,0:T(8,128)S(1)}, u32[]{:S(2)}, u32[]{:S(2)}) collective-permute-start(f32[2,80,512]{2,1,0:T(8,128)S(1)} %get-tuple-element.43), channel_id=1, source_target_pairs={{0,4},{4,0},{1,5},{5,1},{2,6},{6,2},{3,7},{7,3}} | collective-permute-start | bytes 983048 | tf_op jit(solution)/shard_map/ppermute | solution.py:390
  24.2 17.8 %collective-permute-start.5 = (f32[2,80,512]{2,1,0:T(8,128)S(1)}, f32[2,80,512]{2,1,0:T(8,128)S(1)}, u32[]{:S(2)}, u32[]{:S(2)}) collective-permute-start(f32[2,80,512]{2,1,0:T(8,128)S(1)} %get-tuple-element.45), channel_id=1, source_target_pairs={{0,4},{4,0},{1,5},{5,1},{2,6},{6,2},{3,7},{7,3}} | collective-permute-start | bytes 983048 | tf_op jit(solution)/shard_map/ppermute | solution.py:391
  25.6 7.6 %collective-permute-start = (bf16[80,512]{1,0:T(8,128)(2,1)S(1)}, bf16[80,512]{1,0:T(8,128)(2,1)S(1)}, u32[]{:S(2)}, u32[]{:S(2)}) collective-permute-start(bf16[80,512]{1,0:T(8,128)(2,1)S(1)} %get-tuple-element.35), channel_id=1, source_target_pairs={{0,2},{2,0},{1,3},{3,1},{4,6},{6,4},{5,7},{7,5}} | collective-permute-start | bytes 245768 | tf_op jit(solution)/shard_map/ppermute | solution.py:392
  26.9 6.3 %collective-permute-start.1 = (bf16[80,512]{1,0:T(8,128)(2,1)S(1)}, bf16[80,512]{1,0:T(8,128)(2,1)S(1)}, u32[]{:S(2)}, u32[]{:S(2)}) collective-permute-start(bf16[80,512]{1,0:T(8,128)(2,1)S(1)} %get-tuple-element.36), channel_id=1, source_target_pairs={{0,3},{3,0},{1,2},{2,1},{4,7},{7,4},{5,6},{6,5}} | collective-permute-start | bytes 245768 | tf_op jit(solution)/shard_map/ppermute | solution.py:393
  34.2 7.7 %collective-permute-start.4 = (bf16[160,512]{1,0:T(8,128)(2,1)S(1)}, bf16[160,512]{1,0:T(8,128)(2,1)S(1)}, u32[]{:S(2)}, u32[]{:S(2)}) collective-permute-start(bf16[160,512]{1,0:T(8,128)(2,1)S(1)} %shard_map.103.after_ref), channel_id=1, source_target_pairs={{0,2},{2,0},{1,3},{3,1},{4,6},{6,4},{5,7},{7,5}} | collective-permute-start | bytes 491528 | tf_op jit(solution)/shard_map/ppermute | solution.py:423
  35.5 11.2 %collective-permute-start.2 = (bf16[256,512]{1,0:T(8,128)(2,1)S(1)}, bf16[256,512]{1,0:T(8,128)(2,1)S(1)}, u32[]{:S(2)}, u32[]{:S(2)}) collective-permute-start(bf16[256,512]{1,0:T(8,128)(2,1)S(1)} %shard_map.102.after_ref.ymine_ref), channel_id=1, source_target_pairs={{0,4},{4,0},{1,5},{5,1},{2,6},{6,2},{3,7},{7,3}} | collective-permute-start | bytes 786440 | tf_op jit(solution)/shard_map/ppermute | solution.py:421
  43.7 8.4 %collective-permute-start.6 = (bf16[256,512]{1,0:T(8,128)(2,1)S(1)}, bf16[256,512]{1,0:T(8,128)(2,1)S(1)}, u32[]{:S(2)}, u32[]{:S(2)}) collective-permute-start(bf16[256,512]{1,0:T(8,128)(2,1)S(1)} %near_return.1.after_ref.smine_ref), channel_id=1, source_target_pairs={{0,4},{4,0},{1,5},{5,1},{2,6},{6,2},{3,7},{7,3}} | collective-permute-start | bytes 786440 | tf_op jit(solution)/shard_map/ppermute | solution.py:432
  45.0 1.7 %copy-start = (bf16[256,1024]{1,0:T(8,128)(2,1)S(1)}, bf16[256,1024]{1,0:T(8,128)(2,1)}, u32[]{:S(2)}) copy-start(bf16[256,1024]{1,0:T(8,128)(2,1)} %x_ref.1) | copy-start | bytes 1572868
  45.0 1.7 %copy-start.1 = (bf16[256,1024]{1,0:T(8,128)(2,1)S(1)}, bf16[256,1024]{1,0:T(8,128)(2,1)}, u32[]{:S(2)}) copy-start(bf16[256,1024]{1,0:T(8,128)(2,1)} %gy_ref.1) | copy-start | bytes 1572868
  45.0 5.8 %copy-start.2 = (bf16[1024,8]{0,1:T(8,128)(2,1)S(1)}, bf16[1024,8]{0,1:T(8,128)(2,1)}, u32[]{:S(2)}) copy-start(bf16[1024,8]{0,1:T(8,128)(2,1)} %param.8) | copy-start | bytes 49156

commit v3 on v2

--- a/solution.py
+++ b/solution.py
@@ -90,8 +90,8 @@
         near, far, whole = slice(0, blk), slice(blk, 2 * blk), slice(0, 2 * blk)
         small = [pltpu.make_async_copy(src, dst, in_sem.at[k]) for k, (src, dst) in enumerate(
             ((idx_hbm, idx_ref), (x_hbm, x_ref), (wgt_hbm, wgt_ref), (gy_hbm, gy_ref)))]
-        for copy in small:
-            copy.start()
+        small[0].start()
+        small[1].start()
         barrier = enter({"ep": peers[1]}, {"ep": peers[2]}, {"ep": peers[3]}, {"tp": tp_peer})
         loads = {}
         for e in range(2):
@@ -151,8 +151,8 @@
         dispatch_x(1, 0)()
         dispatch_x(0, 1)()
         dispatch_x(1, 1)()
-        for copy in (loads["i", 1], loads["theirs", 1], loads["mine", 0], loads["mine", 1]):
-            copy.start()
+        small[2].start()
+        small[3].start()
 
         def backward(rows, e):
             dyg = dys_ref[e, rows, :]
@@ -177,7 +177,10 @@
             return [jnp.concatenate([both[e][q * cap:(q + 1) * cap] for e in range(2)], axis=0).astype(BF16) for q in range(2)]
 
         arrived(0, 0, xs_ref, x_r)
+        loads["i", 1].start()
         forward(0, 2, 0)
+        for copy in (loads["theirs", 1], loads["mine", 0], loads["mine", 1]):
+            copy.start()
         small[2].wait()
         small[3].wait()
         prob, chosen, gate = gate_of(x_ref[...], wgt_ref[...], hot)

time: 53.1 us -> 53.1 us (level)
  no operation moved by 1% of the time
where the time goes in v3:
time: 53.1 us; the launch traced here: 53 us
  Pallas kernels  44.7 us (84%)
  starting transfers between devices  6.64 us (13%)
  between operations  0.93 us (2%)
  waiting for transfers between devices  0.72 us (1%)
    pallas_call x1, Pallas kernels, local_block(): pl.pallas_call(make_front(n_experts, capacity, cap), out_shape=(sds((le,...  22.9 us
    pallas_call x7, Pallas kernels, local(): pl.pallas_call(kernel, out_shape=out_shape, in_specs=ins, out_specs=outs,...  15.9 us
    pallas_call x1, Pallas kernels, local_block(): pl.pallas_call(router_grad, out_shape=(sds((n, n_experts), BF16), sds((n_...  4.14 us
    pallas_call x1, Pallas kernels, local_block(): pl.pallas_call(make_near_return(cap), out_shape=sds((n, half), BF16), in_...  1.77 us
    ppermute x1, starting transfers between devices, local_block(): snear_recv = lax.ppermute(snear, 'tp', swap)  1.48 us
    ppermute x1, starting transfers between devices, local_block(): sfar_land = lax.ppermute(sblocks, 'ep', across)  1.28 us
    ppermute x1, starting transfers between devices, local_block(): stheirs = lax.ppermute(smine, 'tp', swap)  1.27 us
    ppermute x1, starting transfers between devices, local_block(): yland0 = lax.ppermute(yfar0, 'ep', across)  1.26 us
  transfers between devices with their start and end apart: 7, of which 2 were waited for; matrix products, arithmetic and copies ran while one was open for 0% of the time, Pallas kernels for 40%

profile of v3, /device:TPU:0, one launch (start us, length us, event | category | flops | bytes accessed | tf_op | source)
XLA Modules:
  0.0 53.0 jit_solution(6878596948446854523)
XLA Ops:
  0.6 22.9 %front.1 = (bf16[2,160,2048]{2,1,0:T(8,128)(2,1)S(1)}, bf16[2,160,2048]{2,1,0:T(8,128)(2,1)S(1)}, bf16[2,160,1024]{2,1,0:T(8,128)(2,1)S(1)}, bf16[2,160,1024]{2,...) custom-call(bf16[256,1024]{1,0:T(8,128)(2,1)} %x_ref.1, ...), custom_call_target="tpu_custom_call" | custom-call | tf_op jit(solution)/shard_map/front/pallas_call | solution.py:368
  23.6 0.6 %collective-permute-start.3 = (f32[2,80,512]{2,1,0:T(8,128)S(1)}, f32[2,80,512]{2,1,0:T(8,128)S(1)}, u32[]{:S(2)}, u32[]{:S(2)}) collective-permute-start(f32[2,80,512]{2,1,0:T(8,128)S(1)} %get-tuple-element.43), channel_id=1, source_target_pairs={{0,4},{4,0},{1,5},{5,1},{2,6},{6,2},{3,7},{7,3}} | collective-permute-start | bytes 983048 | tf_op jit(solution)/shard_map/ppermute | solution.py:393
  24.2 1.5 %collective-permute-start.5 = (f32[2,80,512]{2,1,0:T(8,128)S(1)}, f32[2,80,512]{2,1,0:T(8,128)S(1)}, u32[]{:S(2)}, u32[]{:S(2)}) collective-permute-start(f32[2,80,512]{2,1,0:T(8,128)S(1)} %get-tuple-element.45), channel_id=1, source_target_pairs={{0,4},{4,0},{1,5},{5,1},{2,6},{6,2},{3,7},{7,3}} | collective-permute-start | bytes 983048 | tf_op jit(solution)/shard_map/ppermute | solution.py:394
  25.6 1.3 %collective-permute-start = (bf16[80,512]{1,0:T(8,128)(2,1)S(1)}, bf16[80,512]{1,0:T(8,128)(2,1)S(1)}, u32[]{:S(2)}, u32[]{:S(2)}) collective-permute-start(bf16[80,512]{1,0:T(8,128)(2,1)S(1)} %get-tuple-element.35), channel_id=1, source_target_pairs={{0,2},{2,0},{1,3},{3,1},{4,6},{6,4},{5,7},{7,5}} | collective-permute-start | bytes 245768 | tf_op jit(solution)/shard_map/ppermute | solution.py:395
  26.9 0.0 collective-permute-start.1
  26.9 6.3 %shard_map.101 = (f32[2,2048,1024]{2,1,0:T(8,128)}, f32[2,80,512]{2,1,0:T(8,128)S(1)}, f32[2,80,512]{2,1,0:T(8,128)S(1)}) custom-call(bf16[2,160,2048]{2,1,0:T(8,128)(2,1)S(1)} %get-tuple-element.37.h_ref, bf16[2,160,1024]{2,1,0:T(8,128)(2,1)S(1)} %get-tuple-element.38.dys_ref, bf16[2,160,2048]{2,1,0:T(8,128)(2,1)S(1)} %get-tuple-element.39.da_ref.right_ref, ...), custom_call_target="tpu_custom_call" | custom-call | flops 1342177280 | bytes 16777216 | tf_op jit(solution)/shard_map/pallas_call | solution.py:399
  33.2 0.0 collective-permute-done.yfar0_ref
  33.2 0.0 collective-permute-done.1.yfar1_ref
  33.2 0.3 shard_map.102.after_ref.ymine_ref
  33.5 0.6 %collective-permute-done.3.recv_ref = f32[2,80,512]{2,1,0:T(8,128)S(1)} collective-permute-done((f32[2,80,512]{2,1,0:T(8,128)S(1)}, f32[2,80,512]{2,1,0:T(8,128)S(1)}, u32[]{:S(2)}, u32[]{:S(2)}) %collective-permute-start.3) | collective-permute-done | bytes 327712 | tf_op jit(solution)/shard_map/ppermute | solution.py:393
  34.2 1.3 %collective-permute-start.4 = (bf16[160,512]{1,0:T(8,128)(2,1)S(1)}, bf16[160,512]{1,0:T(8,128)(2,1)S(1)}, u32[]{:S(2)}, u32[]{:S(2)}) collective-permute-start(bf16[160,512]{1,0:T(8,128)(2,1)S(1)} %shard_map.103.after_ref), channel_id=1, source_target_pairs={{0,2},{2,0},{1,3},{3,1},{4,6},{6,4},{5,7},{7,5}} | collective-permute-start | bytes 491528 | tf_op jit(solution)/shard_map/ppermute | solution.py:426
  35.5 0.8 %collective-permute-start.2 = (bf16[256,512]{1,0:T(8,128)(2,1)S(1)}, bf16[256,512]{1,0:T(8,128)(2,1)S(1)}, u32[]{:S(2)}, u32[]{:S(2)}) collective-permute-start(bf16[256,512]{1,0:T(8,128)(2,1)S(1)} %shard_map.102.after_ref.ymine_ref), channel_id=1, source_target_pairs={{0,4},{4,0},{1,5},{5,1},{2,6},{6,2},{3,7},{7,3}} | collective-permute-start | bytes 786440 | tf_op jit(solution)/shard_map/ppermute | solution.py:424
  36.3 5.6 %shard_map.104 = (f32[2,1024,2048]{2,1,0:T(8,128)}, f32[8,128]{1,0:T(8,128)S(1)}) custom-call(bf16[2,160,1024]{2,1,0:T(8,128)(2,1)S(1)} %get-tuple-element.42.left_ref, bf16[2,160,2048]{2,1,0:T(8,128)(2,1)S(1)} %get-tuple-element.39.da_ref.right_ref, bf16[160,512]{1,0:T(8,128)(2,1)S(1)} %shard_map.103.after_ref), custom_call_target="tpu_custom_call" | custom-call | flops 1174405120 | bytes 14680064 | tf_op jit(solution)/shard_map/pallas_call | solution.py:399
  41.9 0.0 collective-permute-done.5.srecv_ref
  41.9 0.0 collective-permute-done.4.sfar_ref
  41.9 1.8 %near_return.1.after_ref.smine_ref = bf16[256,512]{1,0:T(8,128)(2,1)S(1)} custom-call(bf16[320,256]{1,0:T(8,128)(2,1)S(1)} %get-tuple-element.33.picks_ref, bf16[160,512]{1,0:T(8,128)(2,1)S(1)} %collective-permute-done.4.sfar_ref, f32[2,80,512]{2,1,0:T(8,128)S(1)} %get-tuple-element.44.sown_ref, f32[2,80,512]{2,1,0:T(8,128)S(1)} %collective-permute-done.5.srecv_ref, ...), custom_call_target="tpu_custom_call" | custom-call | tf_op jit(solution)/shard_map/near_return/pallas_call | solution.py:429
  43.7 1.3 %collective-permute-start.6 = (bf16[256,512]{1,0:T(8,128)(2,1)S(1)}, bf16[256,512]{1,0:T(8,128)(2,1)S(1)}, u32[]{:S(2)}, u32[]{:S(2)}) collective-permute-start(bf16[256,512]{1,0:T(8,128)(2,1)S(1)} %near_return.1.after_ref.smine_ref), channel_id=1, source_target_pairs={{0,4},{4,0},{1,5},{5,1},{2,6},{6,2},{3,7},{7,3}} | collective-permute-start | bytes 786440 | tf_op jit(solution)/shard_map/ppermute | solution.py:435
  45.0 0.0 copy-start
  45.0 0.0 copy-start.1
  45.0 0.0 copy-start.2
  45.0 1.7 %shard_map.105 = (f32[2,1024,2048]{2,1,0:T(8,128)}, f32[8,128]{1,0:T(8,128)S(1)}) custom-call(bf16[2,160,1024]{2,1,0:T(8,128)(2,1)S(1)} %get-tuple-element.42.left_ref, bf16[2,160,2048]{2,1,0:T(8,128)(2,1)S(1)} %get-tuple-element.39.da_ref.right_ref, bf16[256,512]{1,0:T(8,128)(2,1)S(1)} %near_return.1.after_ref.smine_ref, ...), custom_call_target="tpu_custom_call", output_to_operand_aliasing={{0}: (3, {})} | custom-call | flops 167772160 | bytes 2097152 | tf_op jit(solution)/shard_map/pallas_call | solution.py:399
  46.7 0.0 collective-permute-done.2.ytheirs_ref
  46.7 0.0 copy-done
  46.7 0.0 copy-done.1
  46.7 4.1 %router_grad.1 = (bf16[256,8]{1,0:T(8,128)(2,1)S(1)}, f32[8,1024]{1,0:T(8,128)S(1)}) custom-call(bf16[256,1024]{1,0:T(8,128)(2,1)S(1)} %copy-done, bf16[256,1024]{1,0:T(8,128)(2,1)S(1)} %copy-done.1, f32[256,8]{1,0:T(8,128)S(1)} %get-tuple-element.31.prob_ref, f32[256,8]{1,0:T(8,128)S(1)} %get-tuple-element.32.chosen_ref, ...), custom_call_target="tpu_custom_call" | custom-call | tf_op jit(solution)/shard_map/router_grad/pallas_call | solution.py:437
  50.8 0.0 copy-done.2
  50.9 1.2 %shard_map.106 = (bf16[256,1024]{1,0:T(8,128)(2,1)}, f32[8,1024]{1,0:T(8,128)}, bf16[256,1024]{1,0:T(8,128)(2,1)}, f32[256,512]{1,0:T(8,128)S(1)}) custom-call(f32[8,1024]{1,0:T(8,128)S(1)} %get-tuple-element.49.dwgt_ref, bf16[256,512]{1,0:T(8,128)(2,1)S(1)} %shard_map.102.after_ref.ymine_ref, bf16[256,512]{1,0:T(8,128)(2,1)S(1)} %collective-permute-done.2.ytheirs_ref, ...), custom_call_target="tpu_custom_call" | custom-call | tf_op jit(solution)/shard_map/pallas_call | solution.py:399
  52.0 0.1 collective-permute-done.6.stheirs_ref
  52.1 0.8 %shard_map.107 = bf16[256,1024]{1,0:T(8,128)(2,1)} custom-call(f32[256,512]{1,0:T(8,128)S(1)} %get-tuple-element.52.rgrad_ref, bf16[256,512]{1,0:T(8,128)(2,1)S(1)} %collective-permute-done.6.stheirs_ref, bf16[256,1024]{1,0:T(8,128)(2,1)} %get-tuple-element.53.dx_in), custom_call_target="tpu_custom_call", output_to_operand_aliasing={{}: (2, {})} | custom-call | tf_op jit(solution)/shard_map/pallas_call | solution.py:399
  (1 shorter events, 0.0 us)
Async XLA Ops:
  23.6 10.6 %collective-permute-start.3 = (f32[2,80,512]{2,1,0:T(8,128)S(1)}, f32[2,80,512]{2,1,0:T(8,128)S(1)}, u32[]{:S(2)}, u32[]{:S(2)}) collective-permute-start(f32[2,80,512]{2,1,0:T(8,128)S(1)} %get-tuple-element.43), channel_id=1, source_target_pairs={{0,4},{4,0},{1,5},{5,1},{2,6},{6,2},{3,7},{7,3}} | collective-permute-start | bytes 983048 | tf_op jit(solution)/shard_map/ppermute | solution.py:393
  24.2 17.8 %collective-permute-start.5 = (f32[2,80,512]{2,1,0:T(8,128)S(1)}, f32[2,80,512]{2,1,0:T(8,128)S(1)}, u32[]{:S(2)}, u32[]{:S(2)}) collective-permute-start(f32[2,80,512]{2,1,0:T(8,128)S(1)} %get-tuple-element.45), channel_id=1, source_target_pairs={{0,4},{4,0},{1,5},{5,1},{2,6},{6,2},{3,7},{7,3}} | collective-permute-start | bytes 983048 | tf_op jit(solution)/shard_map/ppermute | solution.py:394
  25.6 7.6 %collective-permute-start = (bf16[80,512]{1,0:T(8,128)(2,1)S(1)}, bf16[80,512]{1,0:T(8,128)(2,1)S(1)}, u32[]{:S(2)}, u32[]{:S(2)}) collective-permute-start(bf16[80,512]{1,0:T(8,128)(2,1)S(1)} %get-tuple-element.35), channel_id=1, source_target_pairs={{0,2},{2,0},{1,3},{3,1},{4,6},{6,4},{5,7},{7,5}} | collective-permute-start | bytes 245768 | tf_op jit(solution)/shard_map/ppermute | solution.py:395
  26.9 6.3 %collective-permute-start.1 = (bf16[80,512]{1,0:T(8,128)(2,1)S(1)}, bf16[80,512]{1,0:T(8,128)(2,1)S(1)}, u32[]{:S(2)}, u32[]{:S(2)}) collective-permute-start(bf16[80,512]{1,0:T(8,128)(2,1)S(1)} %get-tuple-element.36), channel_id=1, source_target_pairs={{0,3},{3,0},{1,2},{2,1},{4,7},{7,4},{5,6},{6,5}} | collective-permute-start | bytes 245768 | tf_op jit(solution)/shard_map/ppermute | solution.py:396
  34.2 7.7 %collective-permute-start.4 = (bf16[160,512]{1,0:T(8,128)(2,1)S(1)}, bf16[160,512]{1,0:T(8,128)(2,1)S(1)}, u32[]{:S(2)}, u32[]{:S(2)}) collective-permute-start(bf16[160,512]{1,0:T(8,128)(2,1)S(1)} %shard_map.103.after_ref), channel_id=1, source_target_pairs={{0,2},{2,0},{1,3},{3,1},{4,6},{6,4},{5,7},{7,5}} | collective-permute-start | bytes 491528 | tf_op jit(solution)/shard_map/ppermute | solution.py:426
  35.5 11.2 %collective-permute-start.2 = (bf16[256,512]{1,0:T(8,128)(2,1)S(1)}, bf16[256,512]{1,0:T(8,128)(2,1)S(1)}, u32[]{:S(2)}, u32[]{:S(2)}) collective-permute-start(bf16[256,512]{1,0:T(8,128)(2,1)S(1)} %shard_map.102.after_ref.ymine_ref), channel_id=1, source_target_pairs={{0,4},{4,0},{1,5},{5,1},{2,6},{6,2},{3,7},{7,3}} | collective-permute-start | bytes 786440 | tf_op jit(solution)/shard_map/ppermute | solution.py:424
  43.7 8.4 %collective-permute-start.6 = (bf16[256,512]{1,0:T(8,128)(2,1)S(1)}, bf16[256,512]{1,0:T(8,128)(2,1)S(1)}, u32[]{:S(2)}, u32[]{:S(2)}) collective-permute-start(bf16[256,512]{1,0:T(8,128)(2,1)S(1)} %near_return.1.after_ref.smine_ref), channel_id=1, source_target_pairs={{0,4},{4,0},{1,5},{5,1},{2,6},{6,2},{3,7},{7,3}} | collective-permute-start | bytes 786440 | tf_op jit(solution)/shard_map/ppermute | solution.py:435
  45.0 1.7 %copy-start = (bf16[256,1024]{1,0:T(8,128)(2,1)S(1)}, bf16[256,1024]{1,0:T(8,128)(2,1)}, u32[]{:S(2)}) copy-start(bf16[256,1024]{1,0:T(8,128)(2,1)} %x_ref.1) | copy-start | bytes 1572868
  45.0 1.7 %copy-start.1 = (bf16[256,1024]{1,0:T(8,128)(2,1)S(1)}, bf16[256,1024]{1,0:T(8,128)(2,1)}, u32[]{:S(2)}) copy-start(bf16[256,1024]{1,0:T(8,128)(2,1)} %gy_ref.1) | copy-start | bytes 1572868
  45.0 5.8 %copy-start.2 = (bf16[1024,8]{0,1:T(8,128)(2,1)S(1)}, bf16[1024,8]{0,1:T(8,128)(2,1)}, u32[]{:S(2)}) copy-start(bf16[1024,8]{0,1:T(8,128)(2,1)} %param.8) | copy-start | bytes 49156
